TPU v7x, 32 devices: a whole 2x2x4 slice. The times are simulated.
32 devices in a mesh: row: 4 (over x, core), col: 8 (over z, y).
Axes of the slice: x: 2, y: 2, z: 4, core: 2. Of those that a mesh axis runs over, the one named last changes fastest.
Arguments:
- tokens_in: bfloat16 [8192, 2048], P('row', 'col'), may hold values from -6 to 6
- grad_out: bfloat16 [8192, 2048], P('row', 'col'), may hold values from -6 to 6
- sequence_lengths: int32 [4, 32], P('row'), may hold values from 0 to 2048, as said below
- step_count: int32 [1], replicated, may hold values from 2 to 20
- query_key_value: float32 [2048, 6144], P('row', 'col'), may hold values from -0.1875 to 0.1875
- attn_dense: float32 [2048, 2048], P('col', 'row'), may hold values from -0.5 to 0.5
- mlp_expand: float32 [2048, 8192], P('row', 'col'), may hold values from -0.125 to 0.125
- mlp_reduce: float32 [8192, 2048], P('col', 'row'), may hold values from -0.0625 to 0.0625
- norm_params: float32 [4, 2048], replicated, may hold values from -0.4 to 1.4
- query_bias: float32 [6144], P('col'), may hold values from -0.625 to 0.625
- dense_biases: float32 [2, 2048], P(None, 'col'), may hold values from -0.625 to 0.625
- expand_bias: float32 [8192], P('col'), may hold values from -0.625 to 0.625
- norm_first: float32 [4, 2048], replicated, may hold values from -0.007954951 to 0.007954951
- norm_second: float32 [4, 2048], replicated, may hold values from 2.3071289e-06 to 0.00033325195
- query_bias_first: float32 [6144], P('col'), may hold values from -0.01171875 to 0.01171875
- query_bias_second: float32 [6144], P('col'), may hold values from 1.4404297e-05 to 5.7739257e-05
- dense_biases_first: float32 [2, 2048], P(None, 'col'), may hold values from -0.0078125 to 0.0078125
- dense_biases_second: float32 [2, 2048], P(None, 'col'), may hold values from 6.4208984e-06 to 2.5634765e-05
- expand_bias_first: float32 [8192], P('col'), may hold values from -0.001953125 to 0.001953125
- expand_bias_second: float32 [8192], P('col'), may hold values from 5.7373046e-07 to 2.3193359e-06
- query_left: float32 [16, 48, 128, 128], P('row', 'col'), may hold values from -0.0002624029 to 0.0058139654, as said below
- query_right: float32 [16, 48, 128, 128], P('row', 'col'), may hold values from -0.0002624029 to 0.0058139654, as said below
- attn_left: float32 [16, 16, 128, 128], P('col', 'row'), may hold values from -1.0496116e-05 to 0.000232683616, as said below
- attn_right: float32 [16, 16, 128, 128], P('col', 'row'), may hold values from -1.0496116e-05 to 0.000232683616, as said below
- expand_left: float32 [16, 64, 128, 128], P('row', 'col'), may hold values from -1.0496116e-05 to 0.000232683616, as said below
- expand_right: float32 [16, 64, 128, 128], P('row', 'col'), may hold values from -1.0496116e-05 to 0.000232683616, as said below
- reduce_left: float32 [64, 16, 128, 128], P('col', 'row'), may hold values from -4.1984465e-05 to 0.0009302657, as said below
- reduce_right: float32 [64, 16, 128, 128], P('col', 'row'), may hold values from -4.1984465e-05 to 0.0009302657, as said below
- query_left_root: float32 [16, 48, 128, 128], P('row', 'col'), may hold values from -0.122586672 to 1.50949655, as said below
- query_right_root: float32 [16, 48, 128, 128], P('row', 'col'), may hold values from -0.122586672 to 1.50949655, as said below
- attn_left_root: float32 [16, 16, 128, 128], P('col', 'row'), may hold values from -0.46099982 to 5.6766174, as said below
- attn_right_root: float32 [16, 16, 128, 128], P('col', 'row'), may hold values from -0.46099982 to 5.6766174, as said below
- expand_left_root: float32 [16, 64, 128, 128], P('row', 'col'), may hold values from -0.23049991 to 2.8383087, as said below
- expand_right_root: float32 [16, 64, 128, 128], P('row', 'col'), may hold values from -0.23049991 to 2.8383087, as said below
- reduce_left_root: float32 [64, 16, 128, 128], P('col', 'row'), may hold values from -0.115249955 to 1.41915435, as said below
- reduce_right_root: float32 [64, 16, 128, 128], P('col', 'row'), may hold values from -0.115249955 to 1.41915435, as said below
Outputs:
- block_out: float32 [8192, 2048], P('row', 'col')
- tokens_grad: float32 [8192, 2048], P('row', 'col')
- query_key_value_grad: float32 [2048, 6144], P('row', 'col')
- attn_dense_grad: float32 [2048, 2048], P('col', 'row')
- mlp_expand_grad: float32 [2048, 8192], P('row', 'col')
- mlp_reduce_grad: float32 [8192, 2048], P('col', 'row')
- new_query_key_value: float32 [2048, 6144], P('row', 'col')
- new_attn_dense: float32 [2048, 2048], P('col', 'row')
- new_mlp_expand: float32 [2048, 8192], P('row', 'col')
- new_mlp_reduce: float32 [8192, 2048], P('col', 'row')
- new_query_left: float32 [16, 48, 128, 128], P('row', 'col')
- new_query_right: float32 [16, 48, 128, 128], P('row', 'col')
- new_attn_left: float32 [16, 16, 128, 128], P('col', 'row')
- new_attn_right: float32 [16, 16, 128, 128], P('col', 'row')
- new_expand_left: float32 [16, 64, 128, 128], P('row', 'col')
- new_expand_right: float32 [16, 64, 128, 128], P('row', 'col')
- new_reduce_left: float32 [64, 16, 128, 128], P('col', 'row')
- new_reduce_right: float32 [64, 16, 128, 128], P('col', 'row')
- new_norm_params: float32 [4, 2048], replicated
- new_norm_first: float32 [4, 2048], replicated
- new_norm_second: float32 [4, 2048], replicated
- new_query_bias: float32 [6144], P('col')
- new_query_bias_first: float32 [6144], P('col')
- new_query_bias_second: float32 [6144], P('col')
- new_dense_biases: float32 [2, 2048], P(None, 'col')
- new_dense_biases_first: float32 [2, 2048], P(None, 'col')
- new_dense_biases_second: float32 [2, 2048], P(None, 'col')
- new_expand_bias: float32 [8192], P('col')
- new_expand_bias_first: float32 [8192], P('col')
- new_expand_bias_second: float32 [8192], P('col')
Inputs may be any that keep to these rules, and one draw needn't show every extreme that they name: `sequence_lengths`: in each token block the lengths sum to 2048, nonzero ones first, zeros after. Either one sequence fills the block (in max(1, 1) blocks, drawn from the seed) or sequences of 64 to 256 tokens, multiples of 64, fill it. `query_left`: symmetric blocks. `query_right`: symmetric blocks. `attn_left`: symmetric blocks. `attn_right`: symmetric blocks. `expand_left`: symmetric blocks. `expand_right`: symmetric blocks. `reduce_left`: symmetric blocks. `reduce_right`: symmetric blocks. `query_left_root`: symmetric blocks. `query_right_root`: symmetric blocks. `attn_left_root`: symmetric blocks. `attn_right_root`: symmetric blocks. `expand_left_root`: symmetric blocks. `expand_right_root`: symmetric blocks. `reduce_left_root`: symmetric blocks. `reduce_right_root`: symmetric blocks.
All inputs are finite; a program needn't handle non-finite values.
Results may differ from a plain program's by a relative error of at most 0.012.
The roundings to bfloat16 on the way count: a program that leaves them out, or rounds other values in their place, can miss the bound.
Values may be sent and summed in bfloat16 or wider, within the bound.
A program may use at most 320 MiB of HBM per device.

v0:
```python
import functools
import math

import jax
import jax.numpy as jnp
from jax import lax
from jax.experimental import pallas as pl
from jax.experimental.pallas import tpu as pltpu
from jax.sharding import Mesh, PartitionSpec as P


COL = ("far", "near")
HD = 128
ROT = 32


NORM_EPS = 1e-05
ROPE_BASE = 10000.0
MASKED = -1e30
SHAMPOO_DECAY = 0.95
MATRIX_RATE = 0.5
WEIGHT_DECAY = 0.01
FIRST_DECAY = 0.9
SECOND_DECAY = 0.95
VECTOR_RATE = 0.6
ADAM_EPS = 1e-08

NT = (((1,), (1,)), ((), ()))
TN = (((0,), (0,)), ((), ()))
NN = (((1,), (0,)), ((), ()))
VMEM_BYTES = 60 * 1024 * 1024


def mm(a, b, dims=NN):
    return lax.dot_general(a, b, dims, preferred_element_type=jnp.float32)


def params(*semantics):
    return pltpu.CompilerParams(dimension_semantics=semantics, vmem_limit_bytes=VMEM_BYTES)


def cost(flops, moved, exps=0):
    return pl.CostEstimate(flops=int(flops), bytes_accessed=int(moved), transcendentals=int(exps))


def whole(shape):
    return pl.BlockSpec(
        shape, lambda *_: (0,) * len(shape), pipeline_mode=pl.Buffered(buffer_count=1)
    )


def halves(tile, width, blocks):
    half = blocks // 2
    return [
        pl.BlockSpec((tile, width), lambda i, _: (jnp.minimum(i, half - 1), 0)),
        pl.BlockSpec((tile, width), lambda i, _: (jnp.maximum(i - half, 0), 0)),
    ]


def assemble(near, width, mine, other, panel_ref):
    half = pl.num_programs(0) // 2
    for number in range(2):

        @pl.when((pl.program_id(0) >= half) == bool(number))
        def _():
            for far in range(panel_ref.shape[1] // (2 * width)):
                at = slice(far * width, (far + 1) * width)
                here = pl.multiple_of((2 * far + near) * width, width)
                there = pl.multiple_of((2 * far + 1 - near) * width, width)
                panel_ref[:, pl.ds(here, width)] = mine[number][:, at]
                panel_ref[:, pl.ds(there, width)] = other[number][:, at]


def positions(lengths, number):
    tokens = jnp.arange(number, dtype=jnp.int32)
    endings = jnp.cumsum(lengths, dtype=jnp.int32)
    finished = (endings[None, :] <= tokens[:, None]).astype(jnp.int32)
    return jnp.sum(finished * lengths[None, :], -1, dtype=jnp.int32)


def rotary_tables(places):
    middle = ROT // 2
    indices = jnp.arange(middle, dtype=jnp.float32)
    inverse = jnp.exp(indices * (-2.0 * math.log(ROPE_BASE) / ROT))
    angles = places.astype(jnp.float32)[:, None] * inverse[None, :]
    cosine, sine = jnp.cos(angles), jnp.sin(angles)
    number = places.shape[0]
    ones = jnp.ones((number, HD - ROT), jnp.float32)
    gap = jnp.zeros((number, middle), jnp.float32)
    rest = jnp.zeros((number, HD - ROT), jnp.float32)
    return (
        jnp.concatenate([cosine, cosine, ones], -1),
        jnp.concatenate([-sine, gap, rest], -1),
        jnp.concatenate([gap, sine, rest], -1),
    )


def turn(vectors, own, ahead, behind):
    middle = ROT // 2
    return (
        vectors * own
        + pltpu.roll(vectors, HD - middle, 1) * ahead
        + pltpu.roll(vectors, middle, 1) * behind
    )


def front_kernel(
    share, near_ref, mine_first, mine_second, other_first, other_second,
    norm_ref, wq_ref, qb_ref, own_ref, ahead_ref, behind_ref, we_ref, eb_ref,
    x_ref, one_ref, two_ref, stat_ref, qkv_ref, act_ref, slope_ref,
):
    assemble(
        near_ref[0], share, (mine_first, mine_second), (other_first, other_second), x_ref
    )
    x = x_ref[...].astype(jnp.float32)
    mu = jnp.mean(x, -1, keepdims=True)
    center = x - mu
    inverse = lax.rsqrt(jnp.mean(center * center, -1, keepdims=True) + NORM_EPS)
    normalized = center * inverse
    stat_ref[...] = jnp.concatenate([mu, inverse], -1)
    one = (normalized * norm_ref[0:1] + norm_ref[1:2]).astype(jnp.bfloat16)
    two = (normalized * norm_ref[2:3] + norm_ref[3:4]).astype(jnp.bfloat16)
    one_ref[...] = one
    two_ref[...] = two
    own, ahead, behind = own_ref[...], ahead_ref[...], behind_ref[...]
    for head in range(wq_ref.shape[1] // (3 * HD)):
        cols = slice(head * 3 * HD, (head + 1) * 3 * HD)
        triple = mm(one, wq_ref[:, cols]) + qb_ref[:, cols]
        query = turn(triple[:, :HD], own, ahead, behind)
        key = turn(triple[:, HD : 2 * HD], own, ahead, behind)
        qkv_ref[:, cols] = jnp.concatenate([query, key, triple[:, 2 * HD :]], -1).astype(
            jnp.bfloat16
        )
    width = 256
    for first in range(0, we_ref.shape[1], width):
        cols = slice(first, first + width)
        hidden = mm(two, we_ref[:, cols]) + eb_ref[:, cols]
        phi = 0.5 + 0.5 * lax.erf(hidden * (0.5**0.5))
        act_ref[:, cols] = (hidden * phi).astype(jnp.bfloat16)
        density = jnp.exp(-0.5 * hidden * hidden) * ((0.5 / math.pi) ** 0.5)
        slope_ref[:, cols] = phi + hidden * density


def front(near, share, mine, other, norm_params, wq, qbias, tables, we, ebias):
    tokens, features = 2 * mine[0].shape[0], 2 * mine[0].shape[1]
    tile = 256
    blocks = tokens // tile
    wide, hidden = wq.shape[1], we.shape[1]

    def rows(width):
        return pl.BlockSpec((tile, width), lambda i, _: (i, 0))

    return pl.pallas_call(
        functools.partial(front_kernel, share),
        grid_spec=pltpu.PrefetchScalarGridSpec(
            num_scalar_prefetch=1,
            grid=(blocks,),
        in_specs=[
            *halves(tile, features // 2, blocks),
            *halves(tile, features // 2, blocks),
            whole(norm_params.shape),
            whole(wq.shape),
            whole((1, wide)),
            rows(HD),
            rows(HD),
            rows(HD),
            whole(we.shape),
            whole((1, hidden)),
        ],
        out_specs=[
            rows(features),
            rows(features),
            rows(features),
            rows(2),
            rows(wide),
            rows(hidden),
            rows(hidden),
        ],
        ),
        out_shape=[
            jax.ShapeDtypeStruct((tokens, features), jnp.bfloat16),
            jax.ShapeDtypeStruct((tokens, features), jnp.bfloat16),
            jax.ShapeDtypeStruct((tokens, features), jnp.bfloat16),
            jax.ShapeDtypeStruct((tokens, 2), jnp.float32),
            jax.ShapeDtypeStruct((tokens, wide), jnp.bfloat16),
            jax.ShapeDtypeStruct((tokens, hidden), jnp.bfloat16),
            jax.ShapeDtypeStruct((tokens, hidden), jnp.float32),
        ],
        compiler_params=params("arbitrary"),
        cost_estimate=cost(
            2 * tokens * features * (wide + hidden), tokens * (6 * features + 2 * wide + 6 * hidden)
        ),
        name="front",
    )(near, *mine, *other, norm_params, wq, qbias[None], *tables, we, ebias[None])


def scores(q, k, rows, begin, start):
    raw = mm(q, k, NT) * HD**-0.5
    cols = start + lax.broadcasted_iota(jnp.int32, raw.shape, 1)
    return raw, (cols >= begin) & (cols <= rows)


def attend_kernel(from_ref, q_ref, k_ref, v_ref, begin_ref, out_ref, sum_ref, held):
    tile, span = q_ref.shape[0], held.shape[2]
    block = pl.program_id(1)
    low, high = from_ref[block], (block * tile + tile - 1) // span + 1
    q, begin = q_ref[...], begin_ref[...]
    rows = block * tile + lax.broadcasted_iota(jnp.int32, (tile, 1), 0)

    def first_pass(j, top):
        start = pl.multiple_of(j * span, span)
        raw, allowed = scores(q, k_ref[pl.ds(start, span)], rows, begin, start)
        raw = jnp.where(allowed, raw, MASKED)
        held[j] = raw
        return jnp.maximum(top, jnp.max(raw, -1, keepdims=True))

    top = lax.fori_loop(low, high, first_pass, jnp.full((tile, 1), MASKED, jnp.float32))

    def second_pass(j, carry):
        total, out = carry
        start = pl.multiple_of(j * span, span)
        weights = jnp.exp(held[j] - top)
        total = total + jnp.sum(weights, -1, keepdims=True)
        return total, out + mm(weights.astype(jnp.bfloat16), v_ref[pl.ds(start, span)])

    total, out = lax.fori_loop(
        low,
        high,
        second_pass,
        (jnp.zeros((tile, 1), jnp.float32), jnp.zeros((tile, HD), jnp.float32)),
    )
    out_ref[...] = (out / total).astype(jnp.bfloat16)
    sum_ref[...] = top + jnp.log(total)


def tiles(length):
    return min(256, length), min(512, length)


def attend(qkv, begin):
    length = qkv.shape[0]
    heads = qkv.shape[1] // (3 * HD)
    tile, span = tiles(length)
    grid_spec = pltpu.PrefetchScalarGridSpec(
        num_scalar_prefetch=1,
        grid=(heads, length // tile),
        in_specs=[
            pl.BlockSpec((tile, HD), lambda h, i, _: (i, 3 * h)),
            pl.BlockSpec((length, HD), lambda h, i, _: (0, 3 * h + 1)),
            pl.BlockSpec((length, HD), lambda h, i, _: (0, 3 * h + 2)),
            pl.BlockSpec((tile, 1), lambda h, i, _: (i, 0)),
        ],
        out_specs=[
            pl.BlockSpec((tile, HD), lambda h, i, _: (i, h)),
            pl.BlockSpec((None, tile, 1), lambda h, i, _: (h, i, 0)),
        ],
        scratch_shapes=[pltpu.VMEM((length // span, tile, span), jnp.float32)],
    )
    return pl.pallas_call(
        attend_kernel,
        grid_spec=grid_spec,
        out_shape=[
            jax.ShapeDtypeStruct((length, heads * HD), jnp.bfloat16),
            jax.ShapeDtypeStruct((heads, length, 1), jnp.float32),
        ],
        compiler_params=params("arbitrary", "arbitrary"),
        cost_estimate=cost(4 * heads * length * length * HD, 8 * heads * length * HD, heads * length * length),
        name="attend",
    )(begin[::tile] // span, qkv, qkv, qkv, begin[:, None])


def attend_back_kernel(
    from_ref, q_ref, k_ref, v_ref, grad_ref, begin_ref, sum_ref, own_ref, ahead_ref, behind_ref,
    out_ref, probs, probs_back, key_back, value_back,
):
    tile, span = q_ref.shape[0], probs.shape[2]
    block, blocks = pl.program_id(1), pl.num_programs(1)
    low, high = from_ref[block], (block * tile + tile - 1) // span + 1
    q, grad, begin, logsum = q_ref[...], grad_ref[...], begin_ref[...], sum_ref[...]
    rows = block * tile + lax.broadcasted_iota(jnp.int32, (tile, 1), 0)

    @pl.when(block == 0)
    def _():
        key_back[...] = jnp.zeros_like(key_back)
        value_back[...] = jnp.zeros_like(value_back)

    def first_pass(j, inner):
        start = pl.multiple_of(j * span, span)
        raw, allowed = scores(q, k_ref[pl.ds(start, span)], rows, begin, start)
        weights = jnp.where(allowed, jnp.exp(raw - logsum), 0.0)
        back = mm(grad, v_ref[pl.ds(start, span)], NT)
        probs[j] = weights
        probs_back[j] = back
        return inner + jnp.sum(weights * back, -1, keepdims=True)

    inner = lax.fori_loop(low, high, first_pass, jnp.zeros((tile, 1), jnp.float32))

    def second_pass(j, query_back):
        start = pl.multiple_of(j * span, span)
        weights = probs[j]
        raw_back = (weights * (probs_back[j] - inner) * HD**-0.5).astype(jnp.bfloat16)
        part = pl.ds(start, span)
        key_back[part] += mm(raw_back, q, TN)
        value_back[part] += mm(weights.astype(jnp.bfloat16), grad, TN)
        return query_back + mm(raw_back, k_ref[part])

    query_back = lax.fori_loop(low, high, second_pass, jnp.zeros((tile, HD), jnp.float32))
    here = pl.ds(pl.multiple_of(block * tile, tile), tile)
    query_back = turn(query_back, own_ref[here], -ahead_ref[here], -behind_ref[here])
    out_ref[here, :HD] = query_back.astype(jnp.bfloat16)

    @pl.when(block == blocks - 1)
    def _():
        def finish(i, _):
            at = pl.ds(pl.multiple_of(i * tile, tile), tile)
            keys = turn(key_back[at], own_ref[at], -ahead_ref[at], -behind_ref[at])
            out_ref[at, HD : 2 * HD] = keys.astype(jnp.bfloat16)
            out_ref[at, 2 * HD :] = value_back[at].astype(jnp.bfloat16)
            return 0

        lax.fori_loop(0, blocks, finish, 0)


def attend_back(qkv, begin, grad, logsum, tables):
    length = qkv.shape[0]
    heads = qkv.shape[1] // (3 * HD)
    tile, span = tiles(length)
    grid_spec = pltpu.PrefetchScalarGridSpec(
        num_scalar_prefetch=1,
        grid=(heads, length // tile),
        in_specs=[
            pl.BlockSpec((tile, HD), lambda h, i, _: (i, 3 * h)),
            pl.BlockSpec((length, HD), lambda h, i, _: (0, 3 * h + 1)),
            pl.BlockSpec((length, HD), lambda h, i, _: (0, 3 * h + 2)),
            pl.BlockSpec((tile, HD), lambda h, i, _: (i, h)),
            pl.BlockSpec((tile, 1), lambda h, i, _: (i, 0)),
            pl.BlockSpec((None, tile, 1), lambda h, i, _: (h, i, 0)),
            whole((length, HD)),
            whole((length, HD)),
            whole((length, HD)),
        ],
        out_specs=[pl.BlockSpec((length, 3 * HD), lambda h, i, _: (0, h))],
        scratch_shapes=[
            pltpu.VMEM((length // span, tile, span), jnp.float32),
            pltpu.VMEM((length // span, tile, span), jnp.float32),
            pltpu.VMEM((length, HD), jnp.float32),
            pltpu.VMEM((length, HD), jnp.float32),
        ],
    )
    return pl.pallas_call(
        attend_back_kernel,
        grid_spec=grid_spec,
        out_shape=[jax.ShapeDtypeStruct(qkv.shape, jnp.bfloat16)],
        compiler_params=params("arbitrary", "arbitrary"),
        cost_estimate=cost(10 * heads * length * length * HD, 14 * heads * length * HD, heads * length * length),
        name="attend_back",
    )(begin[::tile] // span, qkv, qkv, qkv, grad, begin[:, None], logsum, *tables)[0]


def join_kernel(
    share, near_ref, a_ref, wa_ref, b_ref, wb_ref,
    keep_first, keep_second, away_first, away_second,
):
    near = near_ref[0]
    a, b = a_ref[...], b_ref[...]
    half = pl.num_programs(0) // 2
    for number, keep_ref, away_ref in (
        (0, keep_first, away_first),
        (1, keep_second, away_second),
    ):

        @pl.when((pl.program_id(0) >= half) == bool(number))
        def _():
            def far(f, _):
                at = pl.ds(pl.multiple_of(f * share, share), share)
                here = pl.ds(pl.multiple_of((2 * f + near) * share, share), share)
                there = pl.ds(pl.multiple_of((2 * f + 1 - near) * share, share), share)
                keep_ref[:, at] = mm(a, wa_ref[:, here]) + mm(b, wb_ref[:, here])
                away = mm(a, wa_ref[:, there]) + mm(b, wb_ref[:, there])
                away_ref[:, at] = away.astype(jnp.bfloat16)
                return 0

            lax.fori_loop(0, keep_ref.shape[1] // share, far, 0, unroll=True)


def join(near, share, a, wa, b, wb):
    tokens, features = a.shape[0], wa.shape[1]
    tile = 256
    blocks = tokens // tile
    half = (tokens // 2, features // 2)
    return pl.pallas_call(
        functools.partial(join_kernel, share),
        grid_spec=pltpu.PrefetchScalarGridSpec(
            num_scalar_prefetch=1,
            grid=(blocks,),
            in_specs=[
                pl.BlockSpec((tile, a.shape[1]), lambda i, _: (i, 0)),
                whole(wa.shape),
                pl.BlockSpec((tile, b.shape[1]), lambda i, _: (i, 0)),
                whole(wb.shape),
            ],
            out_specs=[
                *halves(tile, features // 2, blocks),
                *halves(tile, features // 2, blocks),
            ],
        ),
        out_shape=[
            jax.ShapeDtypeStruct(half, jnp.float32),
            jax.ShapeDtypeStruct(half, jnp.float32),
            jax.ShapeDtypeStruct(half, jnp.bfloat16),
            jax.ShapeDtypeStruct(half, jnp.bfloat16),
        ],
        compiler_params=params("arbitrary"),
        cost_estimate=cost(2 * tokens * features * (a.shape[1] + b.shape[1]), 6 * tokens * features),
        name="join",
    )(near, a, wa, b, wb)


def part_kernel(
    share, near_ref, mine_first, mine_second, other_first, other_second,
    wd_ref, wr_ref, slope_ref, g_ref, att_ref, hid_ref, sum_ref,
):
    assemble(
        near_ref[0], share, (mine_first, mine_second), (other_first, other_second), g_ref
    )
    g = g_ref[...]
    att_ref[...] = mm(g, wd_ref[...], NT).astype(jnp.bfloat16)

    @pl.when(pl.program_id(0) == 0)
    def _():
        sum_ref[...] = jnp.zeros_like(sum_ref)

    width = 256
    for first in range(0, wr_ref.shape[0], width):
        cols = slice(first, first + width)
        back = (mm(g, wr_ref[cols], NT) * slope_ref[:, cols]).astype(jnp.bfloat16)
        hid_ref[:, cols] = back
        sum_ref[:, cols] += jnp.sum(back.astype(jnp.float32), 0, keepdims=True)


def part(near, share, mine, other, wd, wr, slope):
    tokens, features = 2 * mine[0].shape[0], 2 * mine[0].shape[1]
    tile = 256
    blocks = tokens // tile

    def rows(width):
        return pl.BlockSpec((tile, width), lambda i, _: (i, 0))

    return pl.pallas_call(
        functools.partial(part_kernel, share),
        grid_spec=pltpu.PrefetchScalarGridSpec(
            num_scalar_prefetch=1,
            grid=(blocks,),
        in_specs=[
            *halves(tile, features // 2, blocks),
            *halves(tile, features // 2, blocks),
            whole(wd.shape),
            whole(wr.shape),
            rows(wr.shape[0]),
        ],
        out_specs=[
            rows(features),
            rows(wd.shape[0]),
            rows(wr.shape[0]),
            pl.BlockSpec((1, wr.shape[0]), lambda i, _: (0, 0)),
        ],
        ),
        out_shape=[
            jax.ShapeDtypeStruct((tokens, features), jnp.bfloat16),
            jax.ShapeDtypeStruct((tokens, wd.shape[0]), jnp.bfloat16),
            jax.ShapeDtypeStruct((tokens, wr.shape[0]), jnp.bfloat16),
            jax.ShapeDtypeStruct((1, wr.shape[0]), jnp.float32),
        ],
        compiler_params=params("arbitrary"),
        cost_estimate=cost(
            2 * tokens * features * (wd.shape[0] + wr.shape[0]), tokens * (2 * features + 8 * wr.shape[0])
        ),
        name="part",
    )(near, *mine, *other, wd, wr, slope)


def back_kernel(
    share, near_ref, tb_ref, wq_ref, hb_ref, we_ref, x_ref, stat_ref, norm_ref,
    keep_first, keep_second, away_first, away_second, row_ref, col_ref,
):
    near = near_ref[0]
    half = pl.num_programs(0) // 2

    @pl.when(pl.program_id(0) == 0)
    def _():
        col_ref[...] = jnp.zeros_like(col_ref)

    triple_back, hidden_back = tb_ref[...], hb_ref[...]
    mu, inverse = stat_ref[:, 0:1], stat_ref[:, 1:2]

    def block(number, plain, crossed):
        cols = pl.ds(pl.multiple_of(number * share, share), share)
        one = mm(triple_back, wq_ref[cols], NT)
        two = mm(hidden_back, we_ref[cols], NT)
        normalized = (x_ref[:, cols].astype(jnp.float32) - mu) * inverse
        col_ref[:, cols] += jnp.concatenate(
            [
                jnp.sum(one * normalized, 0, keepdims=True),
                jnp.sum(one, 0, keepdims=True),
                jnp.sum(two * normalized, 0, keepdims=True),
                jnp.sum(two, 0, keepdims=True),
            ],
            0,
        )
        both = one * norm_ref[0:1, cols] + two * norm_ref[2:3, cols]
        plain = plain + jnp.sum(both, -1, keepdims=True)
        return both, plain, crossed + jnp.sum(both * normalized, -1, keepdims=True)

    zero = jnp.zeros((tb_ref.shape[0], 1), jnp.float32)
    for number, keep_ref, away_ref in (
        (0, keep_first, away_first),
        (1, keep_second, away_second),
    ):

        @pl.when((pl.program_id(0) >= half) == bool(number))
        def _():
            def far(f, carry):
                at = pl.ds(pl.multiple_of(f * share, share), share)
                both, plain, crossed = block(2 * f + near, *carry)
                keep_ref[:, at] = both
                both, plain, crossed = block(2 * f + 1 - near, plain, crossed)
                away_ref[:, at] = both.astype(jnp.bfloat16)
                return plain, crossed

            plain, crossed = lax.fori_loop(
                0, keep_ref.shape[1] // share, far, (zero, zero), unroll=True
            )
            row_ref[...] = jnp.concatenate([plain, crossed], -1)


def back(near, share, triple_back, wq, hidden_back, we, panel, stats, norm_params):
    tokens, features = panel.shape
    tile = 256
    blocks = tokens // tile
    half = (tokens // 2, features // 2)

    def rows(width):
        return pl.BlockSpec((tile, width), lambda i, _: (i, 0))

    return pl.pallas_call(
        functools.partial(back_kernel, share),
        grid_spec=pltpu.PrefetchScalarGridSpec(
            num_scalar_prefetch=1,
            grid=(blocks,),
            in_specs=[
                rows(wq.shape[1]),
                whole(wq.shape),
                rows(we.shape[1]),
                whole(we.shape),
                rows(features),
                rows(2),
                whole(norm_params.shape),
            ],
            out_specs=[
                *halves(tile, features // 2, blocks),
                *halves(tile, features // 2, blocks),
                rows(2),
                pl.BlockSpec((4, features), lambda i, _: (0, 0)),
            ],
        ),
        out_shape=[
            jax.ShapeDtypeStruct(half, jnp.float32),
            jax.ShapeDtypeStruct(half, jnp.float32),
            jax.ShapeDtypeStruct(half, jnp.bfloat16),
            jax.ShapeDtypeStruct(half, jnp.bfloat16),
            jax.ShapeDtypeStruct((tokens, 2), jnp.float32),
            jax.ShapeDtypeStruct((4, features), jnp.float32),
        ],
        compiler_params=params("arbitrary"),
        cost_estimate=cost(
            2 * tokens * features * (wq.shape[1] + we.shape[1]), tokens * 8 * features
        ),
        name="back",
    )(near, triple_back, wq, hidden_back, we, panel, stats, norm_params)


def shampoo_kernel(scaling, w_ref, g_ref, l_ref, r_ref, p_ref, q_ref, nw_ref, nl_ref, nr_ref):
    size = l_ref.shape[-1]
    for block in range(l_ref.shape[1]):
        cols = slice(block * size, (block + 1) * size)
        grad = (g_ref[:, cols] * scaling).astype(jnp.bfloat16)
        nl_ref[0, block] = SHAMPOO_DECAY * l_ref[0, block] + (1.0 - SHAMPOO_DECAY) * mm(grad, grad, NT)
        nr_ref[0, block] = SHAMPOO_DECAY * r_ref[0, block] + (1.0 - SHAMPOO_DECAY) * mm(grad, grad, TN)
        turned = mm(p_ref[0, block].astype(jnp.bfloat16), grad).astype(jnp.bfloat16)
        step = mm(turned, q_ref[0, block].astype(jnp.bfloat16))
        weight = w_ref[:, cols]
        nw_ref[:, cols] = weight - MATRIX_RATE * (step + WEIGHT_DECAY * weight)


def shampoo(weight, gradient, left_stat, right_stat, left_root, right_root, scaling):
    height, breadth = gradient.shape
    size = left_stat.shape[-1]
    across = breadth // size
    flat = pl.BlockSpec((size, breadth), lambda i: (i, 0))
    cube = pl.BlockSpec((1, across, size, size), lambda i: (i, 0, 0, 0))
    return pl.pallas_call(
        functools.partial(shampoo_kernel, scaling),
        grid=(height // size,),
        in_specs=[flat, flat, cube, cube, cube, cube],
        out_specs=[flat, cube, cube],
        out_shape=[
            jax.ShapeDtypeStruct(weight.shape, jnp.float32),
            jax.ShapeDtypeStruct(left_stat.shape, jnp.float32),
            jax.ShapeDtypeStruct(right_stat.shape, jnp.float32),
        ],
        compiler_params=params("arbitrary"),
        cost_estimate=cost(8 * height * breadth * size, 36 * height * breadth),
    )(weight, gradient, left_stat, right_stat, left_root, right_root)


def swap(value, axis, bit):
    size = lax.axis_size(axis)
    return lax.ppermute(value, axis, [(i, i ^ bit) for i in range(size)])


def gather_row(shard, dim):
    if lax.axis_size("row") != 4:
        return lax.all_gather(shard, "row", axis=dim, tiled=True)
    me = lax.axis_index("row")
    across = swap(shard, "row", 2)
    beside = swap(shard, "row", 1)
    corner = swap(across, "row", 1)
    shape = list(shard.shape)
    step = shape[dim]
    shape[dim] *= 4
    out = jnp.zeros(shape, shard.dtype)
    for bit, piece in ((0, shard), (2, across), (1, beside), (3, corner)):
        out = lax.dynamic_update_slice_in_dim(out, piece, (me ^ bit) * step, dim)
    return out


def scatter_row(value, dim):
    if lax.axis_size("row") != 4:
        return lax.psum_scatter(value, "row", scatter_dimension=dim, tiled=True)
    me = lax.axis_index("row")
    step = value.shape[dim] // 4

    def share(owner):
        return lax.dynamic_slice_in_dim(value, owner * step, step, dim)

    far_beside = swap(share(me ^ 3).astype(jnp.bfloat16), "row", 1)
    near_beside = swap(share(me ^ 1).astype(jnp.bfloat16), "row", 1)
    far = share(me ^ 2) + far_beside.astype(jnp.float32)
    across = swap(far.astype(jnp.bfloat16), "row", 2)
    return share(me) + near_beside.astype(jnp.float32) + across.astype(jnp.float32)


def total(value, axes):
    for axis in axes:
        bit = 1
        while bit < lax.axis_size(axis):
            value = value + swap(value, axis, bit)
            bit *= 2
    return value


def gather_far(value):
    half = value.shape[0] // 2
    return [
        lax.all_gather(value[first : first + half], "far", axis=1, tiled=True)
        for first in (0, half)
    ]


def scatter_far(both):
    return lax.psum_scatter(both, "far", scatter_dimension=1, tiled=True)


def pair_sum(kept, received):
    return (kept + received.astype(jnp.float32)).astype(jnp.bfloat16)


def product(a, b):
    return mm(a, b, TN)


def after(value, *others):
    return lax.optimization_barrier((value, *others))[0]


def adam(vector, moment_one, moment_two, gradient, scaling, counter):
    mean_grad = gradient * scaling
    new_one = FIRST_DECAY * moment_one + (1.0 - FIRST_DECAY) * mean_grad
    new_two = SECOND_DECAY * moment_two + (1.0 - SECOND_DECAY) * mean_grad * mean_grad
    first_hat = new_one / (1.0 - FIRST_DECAY**counter)
    second_hat = new_two / (1.0 - SECOND_DECAY**counter)
    new_vector = vector - VECTOR_RATE * first_hat / (jnp.sqrt(second_hat) + ADAM_EPS)
    return (new_vector, new_one, new_two)


def local(
    tokens_in,
    grad_out,
    sequence_lengths,
    step_count,
    query_key_value,
    attn_dense,
    mlp_expand,
    mlp_reduce,
    norm_params,
    query_bias,
    dense_biases,
    expand_bias,
    norm_first,
    norm_second,
    query_bias_first,
    query_bias_second,
    dense_biases_first,
    dense_biases_second,
    expand_bias_first,
    expand_bias_second,
    query_left,
    query_right,
    attn_left,
    attn_right,
    expand_left,
    expand_right,
    reduce_left,
    reduce_right,
    query_left_root,
    query_right_root,
    attn_left_root,
    attn_right_root,
    expand_left_root,
    expand_right_root,
    reduce_left_root,
    reduce_right_root,
):
    input_mine, cotangent_mine = gather_far(tokens_in), gather_far(grad_out)
    input_other = [swap(piece, "near", 1) for piece in input_mine]
    query_full = gather_row(query_key_value.astype(jnp.bfloat16), 0)
    expand_full = gather_row(mlp_expand.astype(jnp.bfloat16), 0)
    dense_full = gather_row(attn_dense.astype(jnp.bfloat16), 1)
    reduce_full = gather_row(mlp_reduce.astype(jnp.bfloat16), 1)
    row_count, col_width = tokens_in.shape
    features = norm_params.shape[1]
    near = lax.axis_index("near").astype(jnp.int32)[None]
    begin = positions(sequence_lengths[0], row_count)
    tables = rotary_tables(jnp.arange(row_count, dtype=jnp.int32) - begin)
    input_panel, first_in, second_in, stats, qkv, activated, slope = front(
        near, col_width, input_mine, input_other, norm_params,
        query_full, query_bias, tables, expand_full, expand_bias,
    )
    cotangent_other = [
        swap(cotangent_mine[0], "near", 1), swap(after(cotangent_mine[1], stats), "near", 1)
    ]
    attended, logsum = attend(qkv, begin)
    *branches_kept, sent_first, sent_second = join(
        near, col_width, attended, dense_full, activated, reduce_full
    )
    branches_got = [swap(sent_first, "near", 1), swap(sent_second, "near", 1)]
    output_sum = jnp.sum(after(grad_out, sent_first), 0, dtype=jnp.float32)
    cotangent_panel, attended_back, hidden_back, hidden_sum = part(
        near, col_width, cotangent_mine, cotangent_other, dense_full, reduce_full,
        after(slope, sent_first),
    )
    triple_back = attend_back(qkv, begin, attended_back, logsum, tables)
    branch_sum = pair_sum(branches_kept[0], after(branches_got[0], triple_back))
    branch_first = scatter_far(branch_sum)
    *both_kept, sent_first, sent_second, row_sums, norm_grad = back(
        near, col_width, after(triple_back, branch_sum), query_full, hidden_back, expand_full,
        input_panel, stats, norm_params,
    )
    both_got = [swap(sent_first, "near", 1), swap(sent_second, "near", 1)]
    cotangent_late = after(cotangent_panel, sent_first)
    reduce_part = product(activated, cotangent_late)
    reduce_grad = scatter_row(reduce_part, 1)
    dense_part = product(attended, cotangent_late)
    dense_grad = scatter_row(dense_part, 1)
    branch_sum = pair_sum(branches_kept[1], after(branches_got[1], dense_part, reduce_part))
    branch_second = scatter_far(branch_sum)
    expand_part = product(after(second_in, branch_sum), hidden_back)
    expand_grad = scatter_row(expand_part, 0)
    qkv_part = product(after(first_in, branch_sum), triple_back)
    qkv_grad = scatter_row(qkv_part, 0)
    first_sum = pair_sum(both_kept[0], after(both_got[0], qkv_part, expand_part))
    both_first = scatter_far(first_sum)
    lanes = 128
    row_sums = total(row_sums.T.reshape(-1, lanes), ("near", "far")).reshape(2, row_count)
    norm_total = total(norm_grad.reshape(-1, lanes), ("near", "far", "row")).reshape(4, features)
    sums = jnp.concatenate(
        [jnp.sum(triple_back, 0, dtype=jnp.float32), output_sum, hidden_sum[0]]
    )
    sums = total(sums.reshape(-1, lanes), ("row",)).reshape(-1)
    query_bias_total = sums[: query_bias.shape[0]]
    output_total = sums[query_bias.shape[0] : query_bias.shape[0] + col_width]
    dense_total = jnp.stack([output_total, output_total])
    expand_total = sums[query_bias.shape[0] + col_width :]
    norm_slice = (tokens_in.astype(jnp.float32) - stats[:, 0:1]) * stats[:, 1:2]
    scaling = 1.0 / (row_count * lax.axis_size("row"))
    counter = step_count[0].astype(jnp.float32)
    new_dense, new_attn_left, new_attn_right = shampoo(
        attn_dense,
        after(dense_grad, qkv_part, expand_part),
        attn_left,
        attn_right,
        attn_left_root,
        attn_right_root,
        scaling,
    )
    new_reduce, new_reduce_left, new_reduce_right = shampoo(
        mlp_reduce,
        after(reduce_grad, qkv_part, expand_part),
        reduce_left,
        reduce_right,
        reduce_left_root,
        reduce_right_root,
        scaling,
    )
    second_sum = pair_sum(both_kept[1], after(both_got[1], new_dense, new_reduce))
    both_second = scatter_far(second_sum)
    new_qkv, new_query_left, new_query_right = shampoo(
        query_key_value,
        after(qkv_grad, second_sum),
        query_left,
        query_right,
        query_left_root,
        query_right_root,
        scaling,
    )
    new_expand, new_expand_left, new_expand_right = shampoo(
        mlp_expand,
        after(expand_grad, second_sum),
        expand_left,
        expand_right,
        expand_left_root,
        expand_right_root,
        scaling,
    )
    branch_share, both = (
        jnp.concatenate([first, after(second, new_qkv, new_expand)], 0).astype(jnp.float32)
        for first, second in ((branch_first, branch_second), (both_first, both_second))
    )
    block_out = tokens_in.astype(jnp.float32) + branch_share + dense_biases[0] + dense_biases[1]
    mean = (row_sums[0] / features)[:, None]
    cross = (row_sums[1] / features)[:, None]
    tokens_grad = grad_out.astype(jnp.float32) + stats[:, 1:2] * (
        both - mean - norm_slice * cross
    )
    new_norm, new_norm_one, new_norm_two = adam(
        norm_params, norm_first, norm_second, norm_total, scaling, counter
    )
    new_qbias, new_qbias_one, new_qbias_two = adam(
        query_bias, query_bias_first, query_bias_second, query_bias_total, scaling, counter
    )
    new_dbias, new_dbias_one, new_dbias_two = adam(
        dense_biases, dense_biases_first, dense_biases_second, dense_total, scaling, counter
    )
    new_ebias, new_ebias_one, new_ebias_two = adam(
        expand_bias, expand_bias_first, expand_bias_second, expand_total, scaling, counter
    )
    return (
        block_out,
        tokens_grad,
        qkv_grad,
        dense_grad,
        expand_grad,
        reduce_grad,
        new_qkv,
        new_dense,
        new_expand,
        new_reduce,
        new_query_left,
        new_query_right,
        new_attn_left,
        new_attn_right,
        new_expand_left,
        new_expand_right,
        new_reduce_left,
        new_reduce_right,
        new_norm,
        new_norm_one,
        new_norm_two,
        new_qbias,
        new_qbias_one,
        new_qbias_two,
        new_dbias,
        new_dbias_one,
        new_dbias_two,
        new_ebias,
        new_ebias_one,
        new_ebias_two,
    )


def solution(mesh):
    rows, cols = mesh.shape["row"], mesh.shape["col"]
    split = Mesh(mesh.devices.reshape(rows, cols // 2, 2), ("row", *COL))
    return jax.shard_map(
        local,
        mesh=split,
        in_specs=(
            P("row", COL),
            P("row", COL),
            P("row", None),
            P(),
            P("row", COL),
            P(COL, "row"),
            P("row", COL),
            P(COL, "row"),
            P(),
            P(COL),
            P(None, COL),
            P(COL),
            P(),
            P(),
            P(COL),
            P(COL),
            P(None, COL),
            P(None, COL),
            P(COL),
            P(COL),
            P("row", COL, None, None),
            P("row", COL, None, None),
            P(COL, "row", None, None),
            P(COL, "row", None, None),
            P("row", COL, None, None),
            P("row", COL, None, None),
            P(COL, "row", None, None),
            P(COL, "row", None, None),
            P("row", COL, None, None),
            P("row", COL, None, None),
            P(COL, "row", None, None),
            P(COL, "row", None, None),
            P("row", COL, None, None),
            P("row", COL, None, None),
            P(COL, "row", None, None),
            P(COL, "row", None, None),
        ),
        out_specs=(
            P("row", COL),
            P("row", COL),
            P("row", COL),
            P(COL, "row"),
            P("row", COL),
            P(COL, "row"),
            P("row", COL),
            P(COL, "row"),
            P("row", COL),
            P(COL, "row"),
            P("row", COL, None, None),
            P("row", COL, None, None),
            P(COL, "row", None, None),
            P(COL, "row", None, None),
            P("row", COL, None, None),
            P("row", COL, None, None),
            P(COL, "row", None, None),
            P(COL, "row", None, None),
            P(),
            P(),
            P(),
            P(COL),
            P(COL),
            P(COL),
            P(None, COL),
            P(None, COL),
            P(None, COL),
            P(COL),
            P(COL),
            P(COL),
        ),
        check_vma=False,
    )
```

profile of v0, /device:TPU:0, one launch (start us, length us, event | category | flops | bytes accessed | tf_op | source)
XLA Modules:
  0.0 615.4 jit_solution(1281648290941488238)
XLA Ops:
  7.3 2.3 fusion.11
  14.4 3.0 collective-permute-start.5
  18.6 1.6 copy-done.11
  20.2 2.3 collective-permute-start.2
  24.9 3.7 multiply_sine_fusion
  28.7 30.5 %all-gather.5.cloned.1.call-done.mine_first = bf16[1024,1024]{1,0:T(8,128)(2,1)} async-done(((bf16[1024,256]{1,0:T(8,128)(2,1)}), bf16[1024,1024]{1,0:T(8,128)(2,1)}) %all-gather.5.cloned.1.call-update) | async-done | bytes 2097168 | tf_op jit(solution)/shard_map/all_gather | solution.py:665
  60.6 2.5 collective-permute-done.8
  63.2 42.6 %all-gather.7.cloned.1.call-done.mine_second = bf16[1024,1024]{1,0:T(8,128)(2,1)} async-done(((bf16[1024,256]{1,0:T(8,128)(2,1)}), bf16[1024,1024]{1,0:T(8,128)(2,1)}) %all-gather.7.cloned.1.call-update) | async-done | bytes 2097168 | tf_op jit(solution)/shard_map/all_gather | solution.py:665
  107.3 1.9 maximum_maximum_fusion.2
  111.2 2.5 broadcast_in_dim.47
  113.7 1.5 constant_dynamic-update-slice_fusion.3
  122.4 2.3 constant_dynamic-update-slice_fusion.10
  124.6 2.3 constant_dynamic-update-slice_fusion.9
  127.7 3.1 constant_dynamic-update-slice_fusion.8.we_ref
  130.8 11.8 %collective-permute-done.11 = bf16[1024,512]{1,0:T(8,128)(2,1)} collective-permute-done((bf16[1024,512]{1,0:T(8,128)(2,1)}, bf16[1024,512]{1,0:T(8,128)(2,1)}, u32[]{:S(2)}, u32[]{:S(2)}) %collective-permute-start.11) | collective-permute-done | bytes 1048608 | tf_op jit(solution)/shard_map/ppermute | solution.py:618
  143.1 9.2 %all-gather.9.cloned.1.call-done.mine_first = bf16[1024,1024]{1,0:T(8,128)(2,1)} async-done(((bf16[1024,256]{1,0:T(8,128)(2,1)}), bf16[1024,1024]{1,0:T(8,128)(2,1)}) %all-gather.9.cloned.1.call-update) | async-done | bytes 2097168 | tf_op jit(solution)/shard_map/all_gather | solution.py:665
  153.2 1.7 collective-permute-start.15
  155.0 34.1 %front.1 = (bf16[2048,2048]{1,0:T(8,128)(2,1)}, bf16[2048,2048]{1,0:T(8,128)(2,1)}, bf16[2048,2048]{1,0:T(8,128)(2,1)}, f32[2048,2]{1,0:T(8,128)}, bf16[2048,768...) custom-call(s32[1]{0:T(128)} %bitcast.near_ref, ...), custom_call_target="tpu_custom_call" | custom-call | flops 15032385536 | bytes 40894464 | tf_op jit(solution)/shard_map/front/pallas_call | solution.py:153
  189.1 9.8 %all-gather.11.cloned.1.call-done.mine_second = bf16[1024,1024]{1,0:T(8,128)(2,1)} async-done(((bf16[1024,256]{1,0:T(8,128)(2,1)}), bf16[1024,1024]{1,0:T(8,128)(2,1)}) %all-gather.11.cloned.1.call-update) | async-done | bytes 2097168 | tf_op jit(solution)/shard_map/all_gather | solution.py:665
  200.3 1.7 constant_dynamic-update-slice_fusion.5
  202.0 1.7 constant_dynamic-update-slice_fusion.4.wa_ref.wd_ref
  203.7 2.3 constant_dynamic-update-slice_fusion.2
  206.0 2.3 constant_dynamic-update-slice_fusion.1
  208.3 2.4 constant_dynamic-update-slice_fusion.wb_ref.wr_ref
  210.7 19.6 %attend.1 = (bf16[2048,256]{1,0:T(8,128)(2,1)}, f32[2,2048,1]{2,1,0:T(8,128)}) custom-call(s32[8]{0:T(128)} %and_select_fusion.from_ref, bf16[2048,768]{1,0:T(8,128)(2,1)} %get-tuple-element.82.q_ref.k_ref.v_ref, bf16[2048,768]{1,0:T(8,128)(2,1)} %get-tuple-element.82.q_ref.k_ref.v_ref, bf16[2048,768]{1,0:T(8,128)(2,1)} %get-tuple-element.82.q_ref.k_ref.v_ref, ...), custom_call_target="tpu_custom_call" | custom-call | flops 4294967296 | bytes 4194304 | tf_op jit(solution)/shard_map/attend/pallas_call | solution.py:259
  230.3 17.7 %join.1 = (f32[1024,1024]{1,0:T(8,128)}, f32[1024,1024]{1,0:T(8,128)}, bf16[1024,1024]{1,0:T(8,128)(2,1)}, bf16[1024,1024]{1,0:T(8,128)(2,1)}) custom-call(s32[1]{0:T(128)} %bitcast.near_ref, bf16[2048,256]{1,0:T(8,128)(2,1)} %get-tuple-element.83.a_ref, bf16[256,2048]{1,0:T(8,128)(2,1)} %constant_dynamic-update-slice_fusion.4.wa_ref.wd_ref, ...), custom_call_target="tpu_custom_call" | custom-call | flops 10737418240 | bytes 25165824 | tf_op jit(solution)/shard_map/join/pallas_call | solution.py:391
  250.0 20.1 %part.1 = (bf16[2048,2048]{1,0:T(8,128)(2,1)}, bf16[2048,256]{1,0:T(8,128)(2,1)}, bf16[2048,1024]{1,0:T(8,128)(2,1)}, f32[1,1024]{1,0:T(1,128)}) custom-call(s32[1]{0:T(128)} %bitcast.near_ref, bf16[1024,1024]{1,0:T(8,128)(2,1)} %all-gather.9.cloned.1.call-done.mine_first, bf16[1024,1024]{1,0:T(8,128)(2,1)} %all-gather.11.cloned.1.call-done.mine_second, ...), custom_call_target="tpu_custom_call" | custom-call | flops 10737418240 | bytes 25165824 | tf_op jit(solution)/shard_map/part/pallas_call | solution.py:449
  270.2 30.8 %attend_back.1.tb_ref = bf16[2048,768]{1,0:T(8,128)(2,1)} custom-call(s32[8]{0:T(128)} %and_select_fusion.from_ref, bf16[2048,768]{1,0:T(8,128)(2,1)} %get-tuple-element.82.q_ref.k_ref.v_ref, bf16[2048,768]{1,0:T(8,128)(2,1)} %get-tuple-element.82.q_ref.k_ref.v_ref, bf16[2048,768]{1,0:T(8,128)(2,1)} %get-tuple-element.82.q_ref.k_ref.v_ref, ...), custom_call_target="tpu_custom_call" | custom-call | flops 10737418240 | bytes 7340032 | tf_op jit(solution)/shard_map/attend_back/pallas_call | solution.py:350
  301.0 4.3 add_convert_fusion.3
  305.3 28.0 %back.1 = (f32[1024,1024]{1,0:T(8,128)}, f32[1024,1024]{1,0:T(8,128)}, bf16[1024,1024]{1,0:T(8,128)(2,1)}, bf16[1024,1024]{1,0:T(8,128)(2,1)}, f32[2048,2]{1,0:T(8,128)}, /*index=5*/f32[4,2048]{1,0:T(4,128)}) custom-call(s32[1]{0:T(128)} %bitcast.near_ref, bf16[2048,768]{1,0:T(8,128)(2,1)} %attend_back.1.tb_ref, bf16[2048,768]{1,0:T(8,128)(2,1)} %copy-done.13, ...), custom_call_target="tpu_custom_call" | custom-call | flops 15032385536 | bytes 33554432 | tf_op jit(solution)/shard_map/back/pallas_call | solution.py:545
  333.3 5.9 fusion.13
  339.9 11.6 %fusion.14 = f32[1024,2048]{1,0:T(8,128)S(1)} fusion(bf16[2048,1024]{1,0:T(8,128)(2,1)S(1)} %copy-done.34, bf16[2048,2048]{1,0:T(8,128)(2,1)} %get-tuple-element.101), kind=kOutput, calls=%fused_computation.87 | convolution fusion | flops 8589934592 | bytes 20971520 | tf_op jit(solution)/shard_map/dot_general | solution.py:35
  351.5 3.3 copy-done.5
  357.4 3.8 add_convert_fusion.2
  362.3 11.8 %fusion.15 = f32[2048,768]{1,0:T(8,128)} fusion(bf16[2048,2048]{1,0:T(8,128)(2,1)} %get-tuple-element.104, bf16[2048,768]{1,0:T(8,128)(2,1)} %attend_back.1.tb_ref), kind=kOutput, calls=%fused_computation.88 | convolution fusion | flops 6442450944 | bytes 17825792 | tf_op jit(solution)/shard_map/dot_general | solution.py:35
  375.3 24.7 %collective-permute-start.24 = (bf16[256,512]{1,0:T(8,128)(2,1)S(1)}, bf16[256,512]{1,0:T(8,128)(2,1)S(1)}, u32[]{:S(2)}, u32[]{:S(2)}) collective-permute-start(bf16[256,512]{1,0:T(8,128)(2,1)S(1)} %add_convert_fusion.7), channel_id=1, source_target_pairs={{0,16},{8,24},{16,0},{24,8},{1,17},{9,25},{17,1},{25,9},{2,18},{10... | collective-permute-start | bytes 786440 | tf_op jit(solution)/shard_map/ppermute | solution.py:618
  399.9 3.0 add_convert_fusion.5
  403.1 13.5 %fusion.16 = f32[2048,1024]{1,0:T(8,128)} fusion(bf16[2048,2048]{1,0:T(8,128)(2,1)} %get-tuple-element.108, bf16[2048,1024]{1,0:T(8,128)(2,1)S(1)} %copy-done.35), kind=kOutput, calls=%fused_computation.89 | convolution fusion | flops 8589934592 | bytes 20971520 | tf_op jit(solution)/shard_map/dot_general | solution.py:35
  417.5 3.7 shard_map.571
  421.2 8.0 %collective-permute-done.27 = bf16[1024,512]{1,0:T(8,128)(2,1)} collective-permute-done((bf16[1024,512]{1,0:T(8,128)(2,1)}, bf16[1024,512]{1,0:T(8,128)(2,1)}, u32[]{:S(2)}, u32[]{:S(2)}) %collective-permute-start.27) | collective-permute-done | bytes 1048608 | tf_op jit(solution)/shard_map/ppermute | solution.py:618
  429.2 4.0 convert_add_fusion.2.g_ref
  433.2 10.7 %shard_map.572 = (f32[1024,512]{1,0:T(8,128)}, f32[8,4,128,128]{3,2,1,0:T(8,128)}, f32[8,4,128,128]{3,2,1,0:T(8,128)}) custom-call(f32[1024,512]{1,0:T(8,128)} %w_ref.5, f32[1024,512]{1,0:T(8,128)} %convert_add_fusion.2.g_ref, f32[8,4,128,128]{3,2,1,0:T(8,128)} %l_ref.5, f32[8,4,128,128]{3,2,1,0:T(8,128)} %r_ref.5, f32[8,4,128,128]{3,2,1,0:T(8,128)} %p_ref.5, ...), custom_call_target="tpu_custom_call" | custom-call | flops 536870912 | bytes 18874368 | tf_op jit(solution)/shard_map/pallas_call | solution.py:601
  444.0 5.0 add_convert_fusion.1
  450.5 1.7 collective-permute-start.31
  453.0 44.7 %collective-permute-done.31 = bf16[1024,1024]{1,0:T(8,128)(2,1)S(1)} collective-permute-done((bf16[1024,1024]{1,0:T(8,128)(2,1)S(1)}, bf16[1024,1024]{1,0:T(8,128)(2,1)S(1)}, u32[]{:S(2)}, u32[]{:S(2)}) %collective-permute-start.31) | collective-permute-done | bytes 2097184 | tf_op jit(solution)/shard_map/ppermute | solution.py:618
  497.7 4.4 add_convert_fusion
  505.9 3.7 dynamic-slice_convert_fusion.1
  510.0 1.7 collective-permute-start.32
  511.7 2.9 collective-permute-start.41
  514.6 3.2 dynamic-slice_convert_fusion.5
  517.9 1.5 collective-permute-start.35
  520.0 1.8 collective-permute-done.35
  522.8 4.3 collective-permute-done.36
  527.7 3.0 collective-permute-start.34
  530.7 3.6 collective-permute-done.37
  536.9 2.5 add_convert_fusion.6
  540.7 2.9 add_convert_fusion.4
  545.2 15.0 %collective-permute-done.20 = bf16[512,768]{1,0:T(8,128)(2,1)} collective-permute-done((bf16[512,768]{1,0:T(8,128)(2,1)}, bf16[512,768]{1,0:T(8,128)(2,1)}, u32[]{:S(2)}, u32[]{:S(2)}) %collective-permute-start.20) | collective-permute-done | bytes 786464 | tf_op jit(solution)/shard_map/ppermute | solution.py:618
  560.2 3.2 convert_add_fusion.3.g_ref
  563.4 18.5 %collective-permute-done.30 = bf16[512,1024]{1,0:T(8,128)(2,1)} collective-permute-done((bf16[512,1024]{1,0:T(8,128)(2,1)}, bf16[512,1024]{1,0:T(8,128)(2,1)}, u32[]{:S(2)}, u32[]{:S(2)}) %collective-permute-start.30) | collective-permute-done | bytes 1048608 | tf_op jit(solution)/shard_map/ppermute | solution.py:618
  581.9 3.8 convert_add_fusion.1.g_ref
  585.7 7.6 %shard_map.573 = (f32[512,768]{1,0:T(8,128)}, f32[4,6,128,128]{3,2,1,0:T(8,128)}, f32[4,6,128,128]{3,2,1,0:T(8,128)}) custom-call(f32[512,768]{1,0:T(8,128)} %w_ref.6, f32[512,768]{1,0:T(8,128)} %convert_add_fusion.3.g_ref, f32[4,6,128,128]{3,2,1,0:T(8,128)} %l_ref.6, f32[4,6,128,128]{3,2,1,0:T(8,128)} %r_ref.6, f32[4,6,128,128]{3,2,1,0:T(8,128)} %p_ref.6, ...), custom_call_target="tpu_custom_call" | custom-call | flops 402653184 | bytes 14155776 | tf_op jit(solution)/shard_map/pallas_call | solution.py:601
  593.3 9.5 %shard_map.574 = (f32[512,1024]{1,0:T(8,128)}, f32[4,8,128,128]{3,2,1,0:T(8,128)}, f32[4,8,128,128]{3,2,1,0:T(8,128)}) custom-call(f32[512,1024]{1,0:T(8,128)} %w_ref.7, f32[512,1024]{1,0:T(8,128)} %convert_add_fusion.1.g_ref, f32[4,8,128,128]{3,2,1,0:T(8,128)} %l_ref.7, f32[4,8,128,128]{3,2,1,0:T(8,128)} %r_ref.7, f32[4,8,128,128]{3,2,1,0:T(8,128)} %p_ref.7, ...), custom_call_target="tpu_custom_call" | custom-call | flops 536870912 | bytes 18874368 | tf_op jit(solution)/shard_map/pallas_call | solution.py:601
  602.9 5.4 fusion.6
  (213 shorter events, 46.1 us)
Async XLA Ops:
  7.2 52.0 %all-gather.5.cloned.1.call-start = ((), (), s32[]{:S(2)}) async-start(), calls=%async_computation.4 | async-start | bytes 2621440 | tf_op jit(solution)/shard_map/all_gather | solution.py:665
  9.6 96.2 %all-gather.7.cloned.1.call-start = ((), (), s32[]{:S(2)}) async-start(), calls=%async_computation.5 | async-start | bytes 2621440 | tf_op jit(solution)/shard_map/all_gather | solution.py:665
  10.4 142.0 %all-gather.9.cloned.1.call-start = ((), (), s32[]{:S(2)}) async-start(), calls=%async_computation.6 | async-start | bytes 2621440 | tf_op jit(solution)/shard_map/all_gather | solution.py:665
  11.5 187.4 %all-gather.11.cloned.1.call-start = ((), (), s32[]{:S(2)}) async-start(), calls=%async_computation.7 | async-start | bytes 2621440 | tf_op jit(solution)/shard_map/all_gather | solution.py:665
  14.4 96.3 %collective-permute-start.5 = (bf16[512,1024]{1,0:T(8,128)(2,1)}, bf16[512,1024]{1,0:T(8,128)(2,1)}, u32[]{:S(2)}, u32[]{:S(2)}) collective-permute-start(bf16[512,1024]{1,0:T(8,128)(2,1)} %get-tuple-element.153), channel_id=1, source_target_pairs={{0,16},{8,24},{16,0},{24,8},{1,17},{9,25},{17,1},{25,9},{2,18},{10... | collective-permute-start | bytes 3145736 | tf_op jit(solution)/shard_map/ppermute | solution.py:618
  17.4 101.4 %collective-permute-start.6 = (bf16[512,1024]{1,0:T(8,128)(2,1)}, bf16[512,1024]{1,0:T(8,128)(2,1)}, u32[]{:S(2)}, u32[]{:S(2)}) collective-permute-start(bf16[512,1024]{1,0:T(8,128)(2,1)} %get-tuple-element.153), channel_id=1, source_target_pairs={{0,8},{8,0},{16,24},{24,16},{1,9},{9,1},{17,25},{25,17},{2,10},{10... | collective-permute-start | bytes 3145736 | tf_op jit(solution)/shard_map/ppermute | solution.py:618
  20.2 89.1 %collective-permute-start.2 = (bf16[512,768]{1,0:T(8,128)(2,1)}, bf16[512,768]{1,0:T(8,128)(2,1)}, u32[]{:S(2)}, u32[]{:S(2)}) collective-permute-start(bf16[512,768]{1,0:T(8,128)(2,1)} %get-tuple-element.155), channel_id=1, source_target_pairs={{0,16},{8,24},{16,0},{24,8},{1,17},{9,25},{17,1},{25,9},{2,18},{10... | collective-permute-start | bytes 2359304 | tf_op jit(solution)/shard_map/ppermute | solution.py:618
  24.4 38.8 %collective-permute-start.8 = (bf16[256,512]{1,0:T(8,128)(2,1)}, bf16[256,512]{1,0:T(8,128)(2,1)S(1)}, u32[]{:S(2)}, u32[]{:S(2)}) collective-permute-start(bf16[256,512]{1,0:T(8,128)(2,1)} %get-tuple-element.151), channel_id=1, source_target_pairs={{0,16},{8,24},{16,0},{24,8},{1,17},{9,25},{17,1},{25,9},{2,18},{10... | collective-permute-start | bytes 786440 | tf_op jit(solution)/shard_map/ppermute | solution.py:618
  24.4 578.4 %reduce-scatter.7.cloned.1.call-start = ((), (), s32[]{:S(2)}) async-start(), calls=%async_computation.9 | async-start | bytes 2621440 | tf_op jit(solution)/shard_map/reduce_scatter | solution.py:671
  59.2 83.5 %collective-permute-start = (bf16[1024,1024]{1,0:T(8,128)(2,1)}, bf16[1024,1024]{1,0:T(8,128)(2,1)}, u32[]{:S(2)}, u32[]{:S(2)}) collective-permute-start(bf16[1024,1024]{1,0:T(8,128)(2,1)} %all-gather.5.cloned.1.call-done.mine_first), channel_id=1, source_target_pairs={{0,1},{1,0},{2,3},{3,2},{4,5},{5,4},{6,7},{7,6},{8,9},{9,8},{10,11... | collective-permute-start | bytes 6291464 | tf_op jit(solution)/shard_map/ppermute | solution.py:618
  105.8 47.5 %collective-permute-start.1 = (bf16[1024,1024]{1,0:T(8,128)(2,1)}, bf16[1024,1024]{1,0:T(8,128)(2,1)}, u32[]{:S(2)}, u32[]{:S(2)}) collective-permute-start(bf16[1024,1024]{1,0:T(8,128)(2,1)} %all-gather.7.cloned.1.call-done.mine_second), channel_id=1, source_target_pairs={{0,1},{1,0},{2,3},{3,2},{4,5},{5,4},{6,7},{7,6},{8,9},{9,8},{10,11... | collective-permute-start | bytes 6291464 | tf_op jit(solution)/shard_map/ppermute | solution.py:618
  109.3 7.9 %collective-permute-start.3 = (bf16[512,768]{1,0:T(8,128)(2,1)}, bf16[512,768]{1,0:T(8,128)(2,1)}, u32[]{:S(2)}, u32[]{:S(2)}) collective-permute-start(bf16[512,768]{1,0:T(8,128)(2,1)} %get-tuple-element.155), channel_id=1, source_target_pairs={{0,8},{8,0},{16,24},{24,16},{1,9},{9,1},{17,25},{25,17},{2,10},{10... | collective-permute-start | bytes 2359304 | tf_op jit(solution)/shard_map/ppermute | solution.py:618
  110.7 16.9 %collective-permute-start.7 = (bf16[512,1024]{1,0:T(8,128)(2,1)}, bf16[512,1024]{1,0:T(8,128)(2,1)}, u32[]{:S(2)}, u32[]{:S(2)}) collective-permute-start(bf16[512,1024]{1,0:T(8,128)(2,1)} %collective-permute-done.5), channel_id=1, source_target_pairs={{0,8},{8,0},{16,24},{24,16},{1,9},{9,1},{17,25},{25,17},{2,10},{10... | collective-permute-start | bytes 3145736 | tf_op jit(solution)/shard_map/ppermute | solution.py:618
  113.7 6.3 %copy-start.12 = (bf16[2048,768]{1,0:T(8,128)(2,1)S(1)}, bf16[2048,768]{1,0:T(8,128)(2,1)}, u32[]{:S(2)}) copy-start(bf16[2048,768]{1,0:T(8,128)(2,1)} %copy-done.11) | copy-start | bytes 9437188
  117.2 25.4 %collective-permute-start.11 = (bf16[1024,512]{1,0:T(8,128)(2,1)}, bf16[1024,512]{1,0:T(8,128)(2,1)}, u32[]{:S(2)}, u32[]{:S(2)}) collective-permute-start(bf16[1024,512]{1,0:T(8,128)(2,1)} %get-tuple-element.149), channel_id=1, source_target_pairs={{0,16},{8,24},{16,0},{24,8},{1,17},{9,25},{17,1},{25,9},{2,18},{10... | collective-permute-start | bytes 3145736 | tf_op jit(solution)/shard_map/ppermute | solution.py:618
  118.7 8.2 %collective-permute-start.4 = (bf16[512,768]{1,0:T(8,128)(2,1)}, bf16[512,768]{1,0:T(8,128)(2,1)S(1)}, u32[]{:S(2)}, u32[]{:S(2)}) collective-permute-start(bf16[512,768]{1,0:T(8,128)(2,1)} %collective-permute-done.2), channel_id=1, source_target_pairs={{0,8},{8,0},{16,24},{24,16},{1,9},{9,1},{17,25},{25,17},{2,10},{10... | collective-permute-start | bytes 2359304 | tf_op jit(solution)/shard_map/ppermute | solution.py:618
  126.9 79.1 %collective-permute-start.12 = (bf16[1024,512]{1,0:T(8,128)(2,1)}, bf16[1024,512]{1,0:T(8,128)(2,1)}, u32[]{:S(2)}, u32[]{:S(2)}) collective-permute-start(bf16[1024,512]{1,0:T(8,128)(2,1)} %get-tuple-element.149), channel_id=1, source_target_pairs={{0,8},{8,0},{16,24},{24,16},{1,9},{9,1},{17,25},{25,17},{2,10},{10... | collective-permute-start | bytes 3145736 | tf_op jit(solution)/shard_map/ppermute | solution.py:618
  127.6 27.4 %copy-start.13 = (bf16[2048,768]{1,0:T(8,128)(2,1)}, bf16[2048,768]{1,0:T(8,128)(2,1)S(1)}, u32[]{:S(2)}) copy-start(bf16[2048,768]{1,0:T(8,128)(2,1)S(1)} %constant_dynamic-update-slice_fusion.12.wq_ref) | copy-start | bytes 9437188
  127.6 71.3 %collective-permute-start.9 = (bf16[256,512]{1,0:T(8,128)(2,1)}, bf16[256,512]{1,0:T(8,128)(2,1)}, u32[]{:S(2)}, u32[]{:S(2)}) collective-permute-start(bf16[256,512]{1,0:T(8,128)(2,1)} %get-tuple-element.151), channel_id=1, source_target_pairs={{0,8},{8,0},{16,24},{24,16},{1,9},{9,1},{17,25},{25,17},{2,10},{10... | collective-permute-start | bytes 786440 | tf_op jit(solution)/shard_map/ppermute | solution.py:618
  142.6 59.4 %collective-permute-start.10 = (bf16[256,512]{1,0:T(8,128)(2,1)S(1)}, bf16[256,512]{1,0:T(8,128)(2,1)}, u32[]{:S(2)}, u32[]{:S(2)}) collective-permute-start(bf16[256,512]{1,0:T(8,128)(2,1)S(1)} %collective-permute-done.8), channel_id=1, source_target_pairs={{0,8},{8,0},{16,24},{24,16},{1,9},{9,1},{17,25},{25,17},{2,10},{10... | collective-permute-start | bytes 786440 | tf_op jit(solution)/shard_map/ppermute | solution.py:618
  142.6 65.7 %collective-permute-start.13 = (bf16[1024,512]{1,0:T(8,128)(2,1)}, bf16[1024,512]{1,0:T(8,128)(2,1)}, u32[]{:S(2)}, u32[]{:S(2)}) collective-permute-start(bf16[1024,512]{1,0:T(8,128)(2,1)} %collective-permute-done.11), channel_id=1, source_target_pairs={{0,8},{8,0},{16,24},{24,16},{1,9},{9,1},{17,25},{25,17},{2,10},{10... | collective-permute-start | bytes 3145736 | tf_op jit(solution)/shard_map/ppermute | solution.py:618
  153.2 96.8 %collective-permute-start.15 = (bf16[1024,1024]{1,0:T(8,128)(2,1)}, bf16[1024,1024]{1,0:T(8,128)(2,1)}, u32[]{:S(2)}, u32[]{:S(2)}) collective-permute-start(bf16[1024,1024]{1,0:T(8,128)(2,1)} %all-gather.9.cloned.1.call-done.mine_first), channel_id=1, source_target_pairs={{0,1},{1,0},{2,3},{3,2},{4,5},{5,4},{6,7},{7,6},{8,9},{9,8},{10,11... | collective-permute-start | bytes 6291464 | tf_op jit(solution)/shard_map/ppermute | solution.py:618
  198.9 51.2 %collective-permute-start.16 = (bf16[1024,1024]{1,0:T(8,128)(2,1)}, bf16[1024,1024]{1,0:T(8,128)(2,1)}, u32[]{:S(2)}, u32[]{:S(2)}) collective-permute-start(bf16[1024,1024]{1,0:T(8,128)(2,1)} %all-gather.11.cloned.1.call-done.mine_second), channel_id=1, source_target_pairs={{0,1},{1,0},{2,3},{3,2},{4,5},{5,4},{6,7},{7,6},{8,9},{9,8},{10,11... | collective-permute-start | bytes 6291464 | tf_op jit(solution)/shard_map/ppermute | solution.py:618
  248.0 53.0 %collective-permute-start.14 = (bf16[1024,1024]{1,0:T(8,128)(2,1)}, bf16[1024,1024]{1,0:T(8,128)(2,1)S(1)}, u32[]{:S(2)}, u32[]{:S(2)}) collective-permute-start(bf16[1024,1024]{1,0:T(8,128)(2,1)} %get-tuple-element.86), channel_id=1, source_target_pairs={{0,1},{1,0},{2,3},{3,2},{4,5},{5,4},{6,7},{7,6},{8,9},{9,8},{10,11... | collective-permute-start | bytes 6291464 | tf_op jit(solution)/shard_map/ppermute | solution.py:618
  248.6 107.5 %collective-permute-start.17 = (bf16[1024,1024]{1,0:T(8,128)(2,1)}, bf16[1024,1024]{1,0:T(8,128)(2,1)}, u32[]{:S(2)}, u32[]{:S(2)}) collective-permute-start(bf16[1024,1024]{1,0:T(8,128)(2,1)} %get-tuple-element.95), channel_id=1, source_target_pairs={{0,1},{1,0},{2,3},{3,2},{4,5},{5,4},{6,7},{7,6},{8,9},{9,8},{10,11... | collective-permute-start | bytes 6291464 | tf_op jit(solution)/shard_map/ppermute | solution.py:618
  305.2 28.0 %copy-start.14 = (bf16[2048,256]{1,0:T(8,128)(2,1)S(1)}, bf16[2048,256]{1,0:T(8,128)(2,1)}, u32[]{:S(2)}) copy-start(bf16[2048,256]{1,0:T(8,128)(2,1)} %get-tuple-element.83.a_ref) | copy-start | bytes 3145732
  333.2 6.7 %copy-start.34 = (bf16[2048,1024]{1,0:T(8,128)(2,1)S(1)}, bf16[2048,1024]{1,0:T(8,128)(2,1)}, u32[]{:S(2)}) copy-start(bf16[2048,1024]{1,0:T(8,128)(2,1)} %get-tuple-element.84.b_ref) | copy-start | bytes 12582916
  361.2 241.7 %reduce-scatter.11.cloned.1.call-start = ((), (), s32[]{:S(2)}) async-start(), calls=%async_computation.11 | async-start | bytes 2621440 | tf_op jit(solution)/shard_map/reduce_scatter | solution.py:671
  361.7 38.3 %collective-permute-start.26 = (bf16[1024,512]{1,0:T(8,128)(2,1)}, bf16[1024,512]{1,0:T(8,128)(2,1)S(1)}, u32[]{:S(2)}, u32[]{:S(2)}) collective-permute-start(bf16[1024,512]{1,0:T(8,128)(2,1)} %get-tuple-element.159), channel_id=1, source_target_pairs={{0,8},{8,0},{16,24},{24,16},{1,9},{9,1},{17,25},{25,17},{2,10},{10... | collective-permute-start | bytes 3145736 | tf_op jit(solution)/shard_map/ppermute | solution.py:618
  361.7 59.5 %collective-permute-start.25 = (bf16[1024,512]{1,0:T(8,128)(2,1)S(1)}, bf16[1024,512]{1,0:T(8,128)(2,1)}, u32[]{:S(2)}, u32[]{:S(2)}) collective-permute-start(bf16[1024,512]{1,0:T(8,128)(2,1)S(1)} %get-tuple-element.158), channel_id=1, source_target_pairs={{0,8},{8,0},{16,24},{24,16},{1,9},{9,1},{17,25},{25,17},{2,10},{10... | collective-permute-start | bytes 3145736 | tf_op jit(solution)/shard_map/ppermute | solution.py:618
  362.2 12.9 %collective-permute-start.23 = (bf16[256,512]{1,0:T(8,128)(2,1)}, bf16[256,512]{1,0:T(8,128)(2,1)S(1)}, u32[]{:S(2)}, u32[]{:S(2)}) collective-permute-start(bf16[256,512]{1,0:T(8,128)(2,1)} %get-tuple-element.163), channel_id=1, source_target_pairs={{0,8},{8,0},{16,24},{24,16},{1,9},{9,1},{17,25},{25,17},{2,10},{10... | collective-permute-start | bytes 786440 | tf_op jit(solution)/shard_map/ppermute | solution.py:618
  374.1 42.5 %collective-permute-start.22 = (bf16[256,512]{1,0:T(8,128)(2,1)S(1)}, bf16[256,512]{1,0:T(8,128)(2,1)S(1)}, u32[]{:S(2)}, u32[]{:S(2)}) collective-permute-start(bf16[256,512]{1,0:T(8,128)(2,1)S(1)} %get-tuple-element.162), channel_id=1, source_target_pairs={{0,8},{8,0},{16,24},{24,16},{1,9},{9,1},{17,25},{25,17},{2,10},{10... | collective-permute-start | bytes 786440 | tf_op jit(solution)/shard_map/ppermute | solution.py:618
  374.6 69.4 %collective-permute-start.21 = (bf16[1024,1024]{1,0:T(8,128)(2,1)}, bf16[1024,1024]{1,0:T(8,128)(2,1)}, u32[]{:S(2)}, u32[]{:S(2)}) collective-permute-start(bf16[1024,1024]{1,0:T(8,128)(2,1)} %get-tuple-element.106), channel_id=1, source_target_pairs={{0,1},{1,0},{2,3},{3,2},{4,5},{5,4},{6,7},{7,6},{8,9},{9,8},{10,11... | collective-permute-start | bytes 6291464 | tf_op jit(solution)/shard_map/ppermute | solution.py:618
  375.3 27.9 %copy-start.35 = (bf16[2048,1024]{1,0:T(8,128)(2,1)S(1)}, bf16[2048,1024]{1,0:T(8,128)(2,1)}, u32[]{:S(2)}) copy-start(bf16[2048,1024]{1,0:T(8,128)(2,1)} %get-tuple-element.98.hb_ref) | copy-start | bytes 12582916
  375.3 41.4 %collective-permute-start.24 = (bf16[256,512]{1,0:T(8,128)(2,1)S(1)}, bf16[256,512]{1,0:T(8,128)(2,1)S(1)}, u32[]{:S(2)}, u32[]{:S(2)}) collective-permute-start(bf16[256,512]{1,0:T(8,128)(2,1)S(1)} %add_convert_fusion.7), channel_id=1, source_target_pairs={{0,16},{8,24},{16,0},{24,8},{1,17},{9,25},{17,1},{25,9},{2,18},{10... | collective-permute-start | bytes 786440 | tf_op jit(solution)/shard_map/ppermute | solution.py:618
  403.0 26.3 %collective-permute-start.27 = (bf16[1024,512]{1,0:T(8,128)(2,1)}, bf16[1024,512]{1,0:T(8,128)(2,1)}, u32[]{:S(2)}, u32[]{:S(2)}) collective-permute-start(bf16[1024,512]{1,0:T(8,128)(2,1)} %add_convert_fusion.5), channel_id=1, source_target_pairs={{0,16},{8,24},{16,0},{24,8},{1,17},{9,25},{17,1},{25,9},{2,18},{10... | collective-permute-start | bytes 3145736 | tf_op jit(solution)/shard_map/ppermute | solution.py:618
  449.0 153.9 %reduce-scatter.5.cloned.1.call-start = ((), (), s32[]{:S(2)}) async-start(), calls=%async_computation.8 | async-start | bytes 2621440 | tf_op jit(solution)/shard_map/reduce_scatter | solution.py:671
  449.7 153.2 %reduce-scatter.9.cloned.1.call-start = ((), (), s32[]{:S(2)}) async-start(), calls=%async_computation.10 | async-start | bytes 2621440 | tf_op jit(solution)/shard_map/reduce_scatter | solution.py:671
  450.5 47.2 %collective-permute-start.31 = (bf16[1024,1024]{1,0:T(8,128)(2,1)S(1)}, bf16[1024,1024]{1,0:T(8,128)(2,1)S(1)}, u32[]{:S(2)}, u32[]{:S(2)}) collective-permute-start(bf16[1024,1024]{1,0:T(8,128)(2,1)S(1)} %copy-done.33), channel_id=1, source_target_pairs={{0,1},{1,0},{2,3},{3,2},{4,5},{5,4},{6,7},{7,6},{8,9},{9,8},{10,11... | collective-permute-start | bytes 6291464 | tf_op jit(solution)/shard_map/ppermute | solution.py:618
  505.9 5.8 collective-permute-start.40
  509.6 8.3 %copy-start.19 = (f32[4,2048]{1,0:T(4,128)S(1)}, f32[4,2048]{1,0:T(4,128)}, u32[]{:S(2)}) copy-start(f32[4,2048]{1,0:T(4,128)} %get-tuple-element.131) | copy-start | bytes 98308
  509.6 12.5 %copy-start.25 = (f32[1024]{0:T(1024)S(1)}, f32[1024]{0:T(1024)}, u32[]{:S(2)}) copy-start(f32[1024]{0:T(1024)} %param.47) | copy-start | bytes 12292
  509.6 12.5 %copy-start.26 = (f32[1024]{0:T(1024)S(1)}, f32[1024]{0:T(1024)}, u32[]{:S(2)}) copy-start(f32[1024]{0:T(1024)} %param.54) | copy-start | bytes 12292
  509.6 12.5 %copy-start.27 = (f32[1024]{0:T(1024)S(1)}, f32[1024]{0:T(1024)}, u32[]{:S(2)}) copy-start(f32[1024]{0:T(1024)} %param.55) | copy-start | bytes 12292
  509.6 17.5 %copy-start.28 = (f32[768]{0:T(1024)S(1)}, f32[768]{0:T(1024)}, u32[]{:S(2)}) copy-start(f32[768]{0:T(1024)} %param.50) | copy-start | bytes 9220
  509.6 17.5 %copy-start.29 = (f32[768]{0:T(1024)S(1)}, f32[768]{0:T(1024)}, u32[]{:S(2)}) copy-start(f32[768]{0:T(1024)} %param.51) | copy-start | bytes 9220
  510.0 24.3 %copy-start.30 = (f32[2,256]{1,0:T(2,128)S(1)}, f32[2,256]{1,0:T(2,128)}, u32[]{:S(2)}) copy-start(f32[2,256]{1,0:T(2,128)} %param.52) | copy-start | bytes 6148
  510.0 24.3 %copy-start.31 = (f32[2,256]{1,0:T(2,128)S(1)}, f32[2,256]{1,0:T(2,128)}, u32[]{:S(2)}) copy-start(f32[2,256]{1,0:T(2,128)} %param.53) | copy-start | bytes 6148
  510.0 9.9 %collective-permute-start.32 = (f32[32,128]{1,0:T(8,128)S(1)}, f32[32,128]{1,0:T(8,128)S(1)}, u32[]{:S(2)}, u32[]{:S(2)}) collective-permute-start(f32[32,128]{1,0:T(8,128)S(1)} %reshape.162), channel_id=1, source_target_pairs={{0,1},{1,0},{2,3},{3,2},{4,5},{5,4},{6,7},{7,6},{8,9},{9,8},{10,11... | collective-permute-start | bytes 49160 | tf_op jit(solution)/shard_map/ppermute | solution.py:618
  511.7 8.2 %collective-permute-start.41 = (f32[16,128]{1,0:T(8,128)S(1)}, f32[16,128]{1,0:T(8,128)S(1)}, u32[]{:S(2)}, u32[]{:S(2)}) collective-permute-start(f32[16,128]{1,0:T(8,128)S(1)} %fusion.25), channel_id=1, source_target_pairs={{0,16},{8,24},{16,0},{24,8},{1,17},{9,25},{17,1},{25,9},{2,18},{10... | collective-permute-start | bytes 24584 | tf_op jit(solution)/shard_map/ppermute | solution.py:618
  517.9 4.0 collective-permute-start.35
  519.4 21.3 %collective-permute-start.29 = (bf16[512,1024]{1,0:T(8,128)(2,1)}, bf16[512,1024]{1,0:T(8,128)(2,1)S(1)}, u32[]{:S(2)}, u32[]{:S(2)}) collective-permute-start(bf16[512,1024]{1,0:T(8,128)(2,1)} %get-tuple-element.157), channel_id=1, source_target_pairs={{0,8},{8,0},{16,24},{24,16},{1,9},{9,1},{17,25},{25,17},{2,10},{10... | collective-permute-start | bytes 3145736 | tf_op jit(solution)/shard_map/ppermute | solution.py:618
  519.4 44.0 %collective-permute-start.28 = (bf16[512,1024]{1,0:T(8,128)(2,1)S(1)}, bf16[512,1024]{1,0:T(8,128)(2,1)S(1)}, u32[]{:S(2)}, u32[]{:S(2)}) collective-permute-start(bf16[512,1024]{1,0:T(8,128)(2,1)S(1)} %get-tuple-element.156), channel_id=1, source_target_pairs={{0,8},{8,0},{16,24},{24,16},{1,9},{9,1},{17,25},{25,17},{2,10},{10... | collective-permute-start | bytes 3145736 | tf_op jit(solution)/shard_map/ppermute | solution.py:618
  519.9 17.0 %collective-permute-start.19 = (bf16[512,768]{1,0:T(8,128)(2,1)}, bf16[512,768]{1,0:T(8,128)(2,1)S(1)}, u32[]{:S(2)}, u32[]{:S(2)}) collective-permute-start(bf16[512,768]{1,0:T(8,128)(2,1)} %get-tuple-element.161), channel_id=1, source_target_pairs={{0,8},{8,0},{16,24},{24,16},{1,9},{9,1},{17,25},{25,17},{2,10},{10... | collective-permute-start | bytes 2359304 | tf_op jit(solution)/shard_map/ppermute | solution.py:618
  519.9 7.8 %collective-permute-start.33 = (f32[32,128]{1,0:T(8,128)S(1)}, f32[32,128]{1,0:T(8,128)S(1)}, u32[]{:S(2)}, u32[]{:S(2)}) collective-permute-start(f32[32,128]{1,0:T(8,128)S(1)} %add.228), channel_id=1, source_target_pairs={{0,2},{2,0},{4,6},{6,4},{1,3},{3,1},{5,7},{7,5},{8,10},{10,8},{12,... | collective-permute-start | bytes 49160 | tf_op jit(solution)/shard_map/ppermute | solution.py:618
  521.9 5.2 collective-permute-start.36
  527.1 7.2 %collective-permute-start.37 = (f32[64,128]{1,0:T(8,128)S(1)}, f32[64,128]{1,0:T(8,128)S(1)}, u32[]{:S(2)}, u32[]{:S(2)}) collective-permute-start(f32[64,128]{1,0:T(8,128)S(1)} %add.233), channel_id=1, source_target_pairs={{0,4},{2,6},{4,0},{6,2},{1,5},{3,7},{5,1},{7,3},{8,12},{10,14},{12... | collective-permute-start | bytes 98312 | tf_op jit(solution)/shard_map/ppermute | solution.py:618
  527.7 8.3 %collective-permute-start.34 = (f32[32,128]{1,0:T(8,128)S(1)}, f32[32,128]{1,0:T(8,128)S(1)}, u32[]{:S(2)}, u32[]{:S(2)}) collective-permute-start(f32[32,128]{1,0:T(8,128)S(1)} %add.229), channel_id=1, source_target_pairs={{0,4},{2,6},{4,0},{6,2},{1,5},{3,7},{5,1},{7,3},{8,12},{10,14},{12... | collective-permute-start | bytes 49160 | tf_op jit(solution)/shard_map/ppermute | solution.py:618
  534.3 1.8 collective-permute-start.38
  536.1 9.1 %collective-permute-start.18 = (bf16[512,768]{1,0:T(8,128)(2,1)}, bf16[512,768]{1,0:T(8,128)(2,1)}, u32[]{:S(2)}, u32[]{:S(2)}) collective-permute-start(bf16[512,768]{1,0:T(8,128)(2,1)} %get-tuple-element.160), channel_id=1, source_target_pairs={{0,8},{8,0},{16,24},{24,16},{1,9},{9,1},{17,25},{25,17},{2,10},{10... | collective-permute-start | bytes 2359304 | tf_op jit(solution)/shard_map/ppermute | solution.py:618
  536.1 8.3 %collective-permute-start.39 = (f32[64,128]{1,0:T(8,128)S(1)}, f32[64,128]{1,0:T(8,128)S(1)}, u32[]{:S(2)}, u32[]{:S(2)}) collective-permute-start(f32[64,128]{1,0:T(8,128)S(1)} %add.235), channel_id=1, source_target_pairs={{0,16},{8,24},{16,0},{24,8},{1,17},{9,25},{17,1},{25,9},{2,18},{10... | collective-permute-start | bytes 98312 | tf_op jit(solution)/shard_map/ppermute | solution.py:618
  539.4 20.7 %collective-permute-start.20 = (bf16[512,768]{1,0:T(8,128)(2,1)}, bf16[512,768]{1,0:T(8,128)(2,1)}, u32[]{:S(2)}, u32[]{:S(2)}) collective-permute-start(bf16[512,768]{1,0:T(8,128)(2,1)} %add_convert_fusion.6), channel_id=1, source_target_pairs={{0,16},{8,24},{16,0},{24,8},{1,17},{9,25},{17,1},{25,9},{2,18},{10... | collective-permute-start | bytes 2359304 | tf_op jit(solution)/shard_map/ppermute | solution.py:618
  543.6 38.2 %collective-permute-start.30 = (bf16[512,1024]{1,0:T(8,128)(2,1)}, bf16[512,1024]{1,0:T(8,128)(2,1)}, u32[]{:S(2)}, u32[]{:S(2)}) collective-permute-start(bf16[512,1024]{1,0:T(8,128)(2,1)} %add_convert_fusion.4), channel_id=1, source_target_pairs={{0,16},{8,24},{16,0},{24,8},{1,17},{9,25},{17,1},{25,9},{2,18},{10... | collective-permute-start | bytes 3145736 | tf_op jit(solution)/shard_map/ppermute | solution.py:618
  593.3 9.6 %copy-start.6 = (bf16[2048,256]{1,0:T(8,128)(2,1)S(1)}, bf16[2048,256]{1,0:T(8,128)(2,1)}, u32[]{:S(2)}) copy-start(bf16[2048,256]{1,0:T(8,128)(2,1)} %param.36) | copy-start | bytes 3145732
  (22 other events, 67.8 us)
Sparse Core Ops, SparseCore 0:
  10.2 48.9 all-gather.4
  61.3 44.4 all-gather.6
  107.9 44.4 all-gather.8
  154.4 44.4 all-gather.10
  361.3 64.0 reduce-scatter.6
  449.1 43.2 reduce-scatter.10
  494.7 44.9 reduce-scatter.4
  542.5 42.8 reduce-scatter.8
where the time goes:
time: 624 us; the launch traced here: 615 us
  waiting for transfers between devices  206 us (33%)
  Pallas kernels  182 us (29%)
  other arithmetic  59.1 us (9%)
  starting transfers between devices  58.7 us (9%)
  local copies, waits for them, and re-layouts  51.4 us (8%)
  matrix products  42.8 us (7%)
  between operations  15.7 us (3%)
    ppermute x42, waiting for transfers between devices, swap(): return lax.ppermute(value, axis, [(i, i ^ bit) for i in range(size)])  112 us
    all_gather x4, waiting for transfers between devices, gather_far(): lax.all_gather(value[first:first + half], 'far', axis=1, tiled=True)  92.1 us
    ppermute x42, starting transfers between devices, swap(): return lax.ppermute(value, axis, [(i, i ^ bit) for i in range(size)])  57.8 us
    dot_general x4, matrix products, mm(): return lax.dot_general(a, b, dims, preferred_element_type=jnp.float32)  42.8 us
    pallas_call x1, Pallas kernels, front(): pl.pallas_call(functools.partial(front_kernel, share), grid_spec=pltpu.Pr...  34.1 us
    pallas_call x4, Pallas kernels, shampoo(): pl.pallas_call(functools.partial(shampoo_kernel, scaling), grid=(height /...  31.5 us
    pallas_call x1, Pallas kernels, attend_back(): pl.pallas_call(attend_back_kernel, grid_spec=grid_spec, out_shape=[jax.Sh...  30.8 us
    pallas_call x1, Pallas kernels, back(): pl.pallas_call(functools.partial(back_kernel, share), grid_spec=pltpu.Pre...  28 us
  transfers between devices with their start and end apart: 50, of which 15 were waited for; matrix products, arithmetic and copies ran while one was open for 21% of the time, Pallas kernels for 30%

commit v1 on v0

--- a/solution.py
+++ b/solution.py
@@ -200,37 +200,51 @@
     return raw, (cols >= begin) & (cols <= rows)
 
 
-def attend_kernel(from_ref, q_ref, k_ref, v_ref, begin_ref, out_ref, sum_ref, held):
-    tile, span = q_ref.shape[0], held.shape[2]
-    block = pl.program_id(1)
+def columns(head, kind):
+    first = (3 * head + kind) * HD
+    return slice(first, first + HD)
+
+
+def attend_kernel(from_ref, qkv_ref, begin_ref, out_ref, sum_ref, held):
+    tile, span = begin_ref.shape[0], held.shape[3]
+    heads = range(held.shape[0])
+    block = pl.program_id(0)
     low, high = from_ref[block], (block * tile + tile - 1) // span + 1
-    q, begin = q_ref[...], begin_ref[...]
+    begin = begin_ref[...]
+    here = pl.ds(pl.multiple_of(block * tile, tile), tile)
+    queries = [qkv_ref[here, columns(h, 0)] for h in heads]
     rows = block * tile + lax.broadcasted_iota(jnp.int32, (tile, 1), 0)
 
-    def first_pass(j, top):
+    def first_pass(j, tops):
         start = pl.multiple_of(j * span, span)
-        raw, allowed = scores(q, k_ref[pl.ds(start, span)], rows, begin, start)
-        raw = jnp.where(allowed, raw, MASKED)
-        held[j] = raw
-        return jnp.maximum(top, jnp.max(raw, -1, keepdims=True))
-
-    top = lax.fori_loop(low, high, first_pass, jnp.full((tile, 1), MASKED, jnp.float32))
+        part = pl.ds(start, span)
+        out = []
+        for h in heads:
+            raw, allowed = scores(queries[h], qkv_ref[part, columns(h, 1)], rows, begin, start)
+            raw = jnp.where(allowed, raw, MASKED)
+            held[h, j] = raw
+            out.append(jnp.maximum(tops[h], jnp.max(raw, -1, keepdims=True)))
+        return tuple(out)
+
+    least = jnp.full((tile, 1), MASKED, jnp.float32)
+    tops = lax.fori_loop(low, high, first_pass, tuple(least for _ in heads))
 
     def second_pass(j, carry):
-        total, out = carry
-        start = pl.multiple_of(j * span, span)
-        weights = jnp.exp(held[j] - top)
-        total = total + jnp.sum(weights, -1, keepdims=True)
-        return total, out + mm(weights.astype(jnp.bfloat16), v_ref[pl.ds(start, span)])
-
-    total, out = lax.fori_loop(
-        low,
-        high,
-        second_pass,
-        (jnp.zeros((tile, 1), jnp.float32), jnp.zeros((tile, HD), jnp.float32)),
-    )
-    out_ref[...] = (out / total).astype(jnp.bfloat16)
-    sum_ref[...] = top + jnp.log(total)
+        part = pl.ds(pl.multiple_of(j * span, span), span)
+        out = []
+        for h in heads:
+            weights = jnp.exp(held[h, j] - tops[h])
+            total = carry[h][0] + jnp.sum(weights, -1, keepdims=True)
+            mixed = mm(weights.astype(jnp.bfloat16), qkv_ref[part, columns(h, 2)])
+            out.append((total, carry[h][1] + mixed))
+        return tuple(out)
+
+    empty = (jnp.zeros((tile, 1), jnp.float32), jnp.zeros((tile, HD), jnp.float32))
+    done = lax.fori_loop(low, high, second_pass, tuple(empty for _ in heads))
+    for h in heads:
+        total, out = done[h]
+        out_ref[:, h * HD : (h + 1) * HD] = (out / total).astype(jnp.bfloat16)
+        sum_ref[h] = tops[h] + jnp.log(total)
 
 
 def tiles(length):
@@ -243,18 +257,13 @@
     tile, span = tiles(length)
     grid_spec = pltpu.PrefetchScalarGridSpec(
         num_scalar_prefetch=1,
-        grid=(heads, length // tile),
-        in_specs=[
-            pl.BlockSpec((tile, HD), lambda h, i, _: (i, 3 * h)),
-            pl.BlockSpec((length, HD), lambda h, i, _: (0, 3 * h + 1)),
-            pl.BlockSpec((length, HD), lambda h, i, _: (0, 3 * h + 2)),
-            pl.BlockSpec((tile, 1), lambda h, i, _: (i, 0)),
-        ],
+        grid=(length // tile,),
+        in_specs=[whole(qkv.shape), pl.BlockSpec((tile, 1), lambda i, _: (i, 0))],
         out_specs=[
-            pl.BlockSpec((tile, HD), lambda h, i, _: (i, h)),
-            pl.BlockSpec((None, tile, 1), lambda h, i, _: (h, i, 0)),
-        ],
-        scratch_shapes=[pltpu.VMEM((length // span, tile, span), jnp.float32)],
+            pl.BlockSpec((tile, heads * HD), lambda i, _: (i, 0)),
+            pl.BlockSpec((heads, tile, 1), lambda i, _: (0, i, 0)),
+        ],
+        scratch_shapes=[pltpu.VMEM((heads, length // span, tile, span), jnp.float32)],
     )
     return pl.pallas_call(
         attend_kernel,
@@ -263,20 +272,24 @@
             jax.ShapeDtypeStruct((length, heads * HD), jnp.bfloat16),
             jax.ShapeDtypeStruct((heads, length, 1), jnp.float32),
         ],
-        compiler_params=params("arbitrary", "arbitrary"),
+        compiler_params=params("arbitrary"),
         cost_estimate=cost(4 * heads * length * length * HD, 8 * heads * length * HD, heads * length * length),
         name="attend",
-    )(begin[::tile] // span, qkv, qkv, qkv, begin[:, None])
+    )(begin[::tile] // span, qkv, begin[:, None])
 
 
 def attend_back_kernel(
-    from_ref, q_ref, k_ref, v_ref, grad_ref, begin_ref, sum_ref, own_ref, ahead_ref, behind_ref,
+    from_ref, qkv_ref, grad_ref, begin_ref, sum_ref, own_ref, ahead_ref, behind_ref,
     out_ref, probs, probs_back, key_back, value_back,
 ):
-    tile, span = q_ref.shape[0], probs.shape[2]
-    block, blocks = pl.program_id(1), pl.num_programs(1)
+    tile, span = begin_ref.shape[0], probs.shape[3]
+    heads = range(probs.shape[0])
+    block, blocks = pl.program_id(0), pl.num_programs(0)
     low, high = from_ref[block], (block * tile + tile - 1) // span + 1
-    q, grad, begin, logsum = q_ref[...], grad_ref[...], begin_ref[...], sum_ref[...]
+    begin = begin_ref[...]
+    here = pl.ds(pl.multiple_of(block * tile, tile), tile)
+    queries = [qkv_ref[here, columns(h, 0)] for h in heads]
+    grads = [grad_ref[:, h * HD : (h + 1) * HD] for h in heads]
     rows = block * tile + lax.broadcasted_iota(jnp.int32, (tile, 1), 0)
 
     @pl.when(block == 0)
@@ -286,36 +299,45 @@
 
     def first_pass(j, inner):
         start = pl.multiple_of(j * span, span)
-        raw, allowed = scores(q, k_ref[pl.ds(start, span)], rows, begin, start)
-        weights = jnp.where(allowed, jnp.exp(raw - logsum), 0.0)
-        back = mm(grad, v_ref[pl.ds(start, span)], NT)
-        probs[j] = weights
-        probs_back[j] = back
-        return inner + jnp.sum(weights * back, -1, keepdims=True)
-
-    inner = lax.fori_loop(low, high, first_pass, jnp.zeros((tile, 1), jnp.float32))
+        part = pl.ds(start, span)
+        out = []
+        for h in heads:
+            raw, allowed = scores(queries[h], qkv_ref[part, columns(h, 1)], rows, begin, start)
+            weights = jnp.where(allowed, jnp.exp(raw - sum_ref[h]), 0.0)
+            back = mm(grads[h], qkv_ref[part, columns(h, 2)], NT)
+            probs[h, j] = weights
+            probs_back[h, j] = back
+            out.append(inner[h] + jnp.sum(weights * back, -1, keepdims=True))
+        return tuple(out)
+
+    zero = jnp.zeros((tile, 1), jnp.float32)
+    inner = lax.fori_loop(low, high, first_pass, tuple(zero for _ in heads))
 
     def second_pass(j, query_back):
-        start = pl.multiple_of(j * span, span)
-        weights = probs[j]
-        raw_back = (weights * (probs_back[j] - inner) * HD**-0.5).astype(jnp.bfloat16)
-        part = pl.ds(start, span)
-        key_back[part] += mm(raw_back, q, TN)
-        value_back[part] += mm(weights.astype(jnp.bfloat16), grad, TN)
-        return query_back + mm(raw_back, k_ref[part])
-
-    query_back = lax.fori_loop(low, high, second_pass, jnp.zeros((tile, HD), jnp.float32))
-    here = pl.ds(pl.multiple_of(block * tile, tile), tile)
-    query_back = turn(query_back, own_ref[here], -ahead_ref[here], -behind_ref[here])
-    out_ref[here, :HD] = query_back.astype(jnp.bfloat16)
+        part = pl.ds(pl.multiple_of(j * span, span), span)
+        out = []
+        for h in heads:
+            weights = probs[h, j]
+            raw_back = (weights * (probs_back[h, j] - inner[h]) * HD**-0.5).astype(jnp.bfloat16)
+            key_back[h, part] += mm(raw_back, queries[h], TN)
+            value_back[h, part] += mm(weights.astype(jnp.bfloat16), grads[h], TN)
+            out.append(query_back[h] + mm(raw_back, qkv_ref[part, columns(h, 1)]))
+        return tuple(out)
+
+    empty = jnp.zeros((tile, HD), jnp.float32)
+    query_back = lax.fori_loop(low, high, second_pass, tuple(empty for _ in heads))
+    for h in heads:
+        turned = turn(query_back[h], own_ref[here], -ahead_ref[here], -behind_ref[here])
+        out_ref[here, columns(h, 0)] = turned.astype(jnp.bfloat16)
 
     @pl.when(block == blocks - 1)
     def _():
         def finish(i, _):
             at = pl.ds(pl.multiple_of(i * tile, tile), tile)
-            keys = turn(key_back[at], own_ref[at], -ahead_ref[at], -behind_ref[at])
-            out_ref[at, HD : 2 * HD] = keys.astype(jnp.bfloat16)
-            out_ref[at, 2 * HD :] = value_back[at].astype(jnp.bfloat16)
+            for h in heads:
+                keys = turn(key_back[h, at], own_ref[at], -ahead_ref[at], -behind_ref[at])
+                out_ref[at, columns(h, 1)] = keys.astype(jnp.bfloat16)
+                out_ref[at, columns(h, 2)] = value_back[h, at].astype(jnp.bfloat16)
             return 0
 
         lax.fori_loop(0, blocks, finish, 0)
@@ -327,34 +349,32 @@
     tile, span = tiles(length)
     grid_spec = pltpu.PrefetchScalarGridSpec(
         num_scalar_prefetch=1,
-        grid=(heads, length // tile),
+        grid=(length // tile,),
         in_specs=[
-            pl.BlockSpec((tile, HD), lambda h, i, _: (i, 3 * h)),
-            pl.BlockSpec((length, HD), lambda h, i, _: (0, 3 * h + 1)),
-            pl.BlockSpec((length, HD), lambda h, i, _: (0, 3 * h + 2)),
-            pl.BlockSpec((tile, HD), lambda h, i, _: (i, h)),
-            pl.BlockSpec((tile, 1), lambda h, i, _: (i, 0)),
-            pl.BlockSpec((None, tile, 1), lambda h, i, _: (h, i, 0)),
+            whole(qkv.shape),
+            pl.BlockSpec((tile, heads * HD), lambda i, _: (i, 0)),
+            pl.BlockSpec((tile, 1), lambda i, _: (i, 0)),
+            pl.BlockSpec((heads, tile, 1), lambda i, _: (0, i, 0)),
             whole((length, HD)),
             whole((length, HD)),
             whole((length, HD)),
         ],
-        out_specs=[pl.BlockSpec((length, 3 * HD), lambda h, i, _: (0, h))],
+        out_specs=[pl.BlockSpec(qkv.shape, lambda i, _: (0, 0))],
         scratch_shapes=[
-            pltpu.VMEM((length // span, tile, span), jnp.float32),
-            pltpu.VMEM((length // span, tile, span), jnp.float32),
-            pltpu.VMEM((length, HD), jnp.float32),
-            pltpu.VMEM((length, HD), jnp.float32),
+            pltpu.VMEM((heads, length // span, tile, span), jnp.float32),
+            pltpu.VMEM((heads, length // span, tile, span), jnp.float32),
+            pltpu.VMEM((heads, length, HD), jnp.float32),
+            pltpu.VMEM((heads, length, HD), jnp.float32),
         ],
     )
     return pl.pallas_call(
         attend_back_kernel,
         grid_spec=grid_spec,
         out_shape=[jax.ShapeDtypeStruct(qkv.shape, jnp.bfloat16)],
-        compiler_params=params("arbitrary", "arbitrary"),
+        compiler_params=params("arbitrary"),
         cost_estimate=cost(10 * heads * length * length * HD, 14 * heads * length * HD, heads * length * length),
         name="attend_back",
-    )(begin[::tile] // span, qkv, qkv, qkv, grad, begin[:, None], logsum, *tables)[0]
+    )(begin[::tile] // span, qkv, grad, begin[:, None], logsum, *tables)[0]
 
 
 def join_kernel(
@@ -743,7 +763,7 @@
     begin = positions(sequence_lengths[0], row_count)
     tables = rotary_tables(jnp.arange(row_count, dtype=jnp.int32) - begin)
     input_panel, first_in, second_in, stats, qkv, activated, slope = front(
-        near, col_width, input_mine, input_other, norm_params,
+        after(near, dense_full, reduce_full), col_width, input_mine, input_other, norm_params,
         query_full, query_bias, tables, expand_full, expand_bias,
     )
     cotangent_other = [
@@ -776,10 +796,10 @@
     branch_second = scatter_far(branch_sum)
     expand_part = product(after(second_in, branch_sum), hidden_back)
     expand_grad = scatter_row(expand_part, 0)
-    qkv_part = product(after(first_in, branch_sum), triple_back)
+    first_sum = pair_sum(both_kept[0], after(both_got[0], expand_part))
+    both_first = scatter_far(first_sum)
+    qkv_part = product(after(first_in, first_sum), triple_back)
     qkv_grad = scatter_row(qkv_part, 0)
-    first_sum = pair_sum(both_kept[0], after(both_got[0], qkv_part, expand_part))
-    both_first = scatter_far(first_sum)
     lanes = 128
     row_sums = total(row_sums.T.reshape(-1, lanes), ("near", "far")).reshape(2, row_count)
     norm_total = total(norm_grad.reshape(-1, lanes), ("near", "far", "row")).reshape(4, features)
@@ -832,10 +852,10 @@
         expand_right_root,
         scaling,
     )
-    branch_share, both = (
-        jnp.concatenate([first, after(second, new_qkv, new_expand)], 0).astype(jnp.float32)
-        for first, second in ((branch_first, branch_second), (both_first, both_second))
-    )
+    branch_share = jnp.concatenate([branch_first, after(branch_second, new_qkv)], 0)
+    branch_share = branch_share.astype(jnp.float32)
+    both = jnp.concatenate([both_first, after(both_second, new_qkv, new_expand)], 0)
+    both = both.astype(jnp.float32)
     block_out = tokens_in.astype(jnp.float32) + branch_share + dense_biases[0] + dense_biases[1]
     mean = (row_sums[0] / features)[:, None]
     cross = (row_sums[1] / features)[:, None]

time: 624 us -> 605 us (0.970)
  Pallas kernels: 182 us -> 170 us
  waiting for transfers between devices: 206 us -> 217 us
  starting transfers between devices: 58.7 us -> 49.1 us
  local copies, waits for them, and re-layouts: 51.4 us -> 44.1 us
    reduce_scatter x4, waiting for transfers between devices: 0.07 us -> 44.5 us  [scatter_far(): return lax.psum_scatter(both, 'far', scatter_dimension=1, tiled=True)]
    ppermute x42, waiting for transfers between devices: 112 us -> 79 us  [swap(): return lax.ppermute(value, axis, [(i, i ^ bit) for i in range(size)])]
    ppermute x42, starting transfers between devices: 57.8 us -> 48.6 us  [swap(): return lax.ppermute(value, axis, [(i, i ^ bit) for i in range(size)])]
    unnamed x72 -> x76, local copies, waits for them, and re-layouts: 10.9 us -> 3.38 us
    pallas_call x1, Pallas kernels: 30.8 us -> 24.5 us  [attend_back(): pl.pallas_call(attend_back_kernel, grid_spec=grid_spec, out_shape=[jax.Sh...]
  transfers between devices with their start and end apart: 50 -> 50, of which waited for: 15 -> 17; matrix products, arithmetic and copies ran while one was open for 21% -> 22% of each run, Pallas kernels for 30% -> 29%
where the time goes in v1:
time: 605 us; the launch traced here: 597 us
  waiting for transfers between devices  217 us (36%)
  Pallas kernels  170 us (28%)
  other arithmetic  60.2 us (10%)
  starting transfers between devices  49.1 us (8%)
  local copies, waits for them, and re-layouts  44.1 us (7%)
  matrix products  40.4 us (7%)
  between operations  15.7 us (3%)
    all_gather x4, waiting for transfers between devices, gather_far(): lax.all_gather(value[first:first + half], 'far', axis=1, tiled=True)  92 us
    ppermute x42, waiting for transfers between devices, swap(): return lax.ppermute(value, axis, [(i, i ^ bit) for i in range(size)])  79 us
    ppermute x42, starting transfers between devices, swap(): return lax.ppermute(value, axis, [(i, i ^ bit) for i in range(size)])  48.6 us
    reduce_scatter x4, waiting for transfers between devices, scatter_far(): return lax.psum_scatter(both, 'far', scatter_dimension=1, tiled=True)  44.5 us
    dot_general x4, matrix products, mm(): return lax.dot_general(a, b, dims, preferred_element_type=jnp.float32)  40.4 us
    pallas_call x1, Pallas kernels, front(): pl.pallas_call(functools.partial(front_kernel, share), grid_spec=pltpu.Pr...  34.1 us
    pallas_call x4, Pallas kernels, shampoo(): pl.pallas_call(functools.partial(shampoo_kernel, scaling), grid=(height /...  31.7 us
    pallas_call x1, Pallas kernels, back(): pl.pallas_call(functools.partial(back_kernel, share), grid_spec=pltpu.Pre...  27.9 us
  transfers between devices with their start and end apart: 50, of which 17 were waited for; matrix products, arithmetic and copies ran while one was open for 22% of the time, Pallas kernels for 29%

profile of v1, /device:TPU:0, one launch (start us, length us, event | category | flops | bytes accessed | tf_op | source)
XLA Modules:
  0.0 596.9 jit_solution(7482619171305015846)
XLA Ops:
  7.3 2.3 fusion.11
  12.4 3.0 collective-permute-start
  16.6 1.7 copy-done.11
  19.5 2.6 broadcast_in_dim.40
  22.1 1.5 constant_dynamic-update-slice_fusion.11
  24.8 2.5 broadcast_in_dim.46
  27.3 1.6 constant_dynamic-update-slice_fusion.3
  31.9 7.3 %collective-permute-done.8 = bf16[512,768]{1,0:T(8,128)(2,1)S(1)} collective-permute-done((bf16[512,768]{1,0:T(8,128)(2,1)}, bf16[512,768]{1,0:T(8,128)(2,1)S(1)}, u32[]{:S(2)}, u32[]{:S(2)}) %collective-permute-start.8) | collective-permute-done | bytes 786464 | tf_op jit(solution)/shard_map/ppermute | solution.py:638
  40.1 3.7 multiply_sine_fusion
  44.0 15.2 %all-gather.5.cloned.1.call-done.mine_first = bf16[1024,1024]{1,0:T(8,128)(2,1)} async-done(((bf16[1024,256]{1,0:T(8,128)(2,1)}), bf16[1024,1024]{1,0:T(8,128)(2,1)}) %all-gather.5.cloned.1.call-update) | async-done | bytes 2097168 | tf_op jit(solution)/shard_map/all_gather | solution.py:685
  61.7 44.1 %all-gather.7.cloned.1.call-done.mine_second = bf16[1024,1024]{1,0:T(8,128)(2,1)} async-done(((bf16[1024,256]{1,0:T(8,128)(2,1)}), bf16[1024,1024]{1,0:T(8,128)(2,1)}) %all-gather.7.cloned.1.call-update) | async-done | bytes 2097168 | tf_op jit(solution)/shard_map/all_gather | solution.py:685
  107.3 2.5 maximum_maximum_fusion.2
  111.2 1.7 constant_dynamic-update-slice_fusion.13
  112.8 1.7 constant_dynamic-update-slice_fusion.12.wa_ref.wd_ref
  116.1 2.1 constant_dynamic-update-slice_fusion.5
  118.2 2.3 constant_dynamic-update-slice_fusion.10
  120.5 2.3 constant_dynamic-update-slice_fusion.2
  122.8 2.3 constant_dynamic-update-slice_fusion.9
  125.1 2.3 constant_dynamic-update-slice_fusion.1
  130.5 21.9 %all-gather.9.cloned.1.call-done.mine_first = bf16[1024,1024]{1,0:T(8,128)(2,1)} async-done(((bf16[1024,256]{1,0:T(8,128)(2,1)}), bf16[1024,1024]{1,0:T(8,128)(2,1)}) %all-gather.9.cloned.1.call-update) | async-done | bytes 2097168 | tf_op jit(solution)/shard_map/all_gather | solution.py:685
  153.9 34.1 %front.1 = (bf16[2048,2048]{1,0:T(8,128)(2,1)}, bf16[2048,2048]{1,0:T(8,128)(2,1)}, bf16[2048,2048]{1,0:T(8,128)(2,1)}, f32[2048,2]{1,0:T(8,128)}, bf16[2048,768...) custom-call(s32[1]{0:T(128)} %bitcast.near_ref, ...), custom_call_target="tpu_custom_call" | custom-call | flops 15032385536 | bytes 40894464 | tf_op jit(solution)/shard_map/front/pallas_call | solution.py:153
  188.0 10.9 %all-gather.11.cloned.1.call-done.mine_second = bf16[1024,1024]{1,0:T(8,128)(2,1)} async-done(((bf16[1024,256]{1,0:T(8,128)(2,1)}), bf16[1024,1024]{1,0:T(8,128)(2,1)}) %all-gather.11.cloned.1.call-update) | async-done | bytes 2097168 | tf_op jit(solution)/shard_map/all_gather | solution.py:685
  202.3 14.2 %attend.1 = (bf16[2048,256]{1,0:T(8,128)(2,1)}, f32[2,2048,1]{2,1,0:T(8,128)}) custom-call(s32[8]{0:T(128)} %and_select_fusion.from_ref, bf16[2048,768]{1,0:T(8,128)(2,1)} %get-tuple-element.84.qkv_ref, s32[2048,1]{1,0:T(8,128)} %copy.77.begin_ref), custom_call_target="tpu_custom_call" | custom-call | flops 4294967296 | bytes 4194304 | tf_op jit(solution)/shard_map/attend/pallas_call | solution.py:268
  216.5 17.7 %join.1 = (f32[1024,1024]{1,0:T(8,128)}, f32[1024,1024]{1,0:T(8,128)}, bf16[1024,1024]{1,0:T(8,128)(2,1)}, bf16[1024,1024]{1,0:T(8,128)(2,1)}) custom-call(s32[1]{0:T(128)} %bitcast.near_ref, bf16[2048,256]{1,0:T(8,128)(2,1)} %get-tuple-element.85.a_ref, bf16[256,2048]{1,0:T(8,128)(2,1)} %constant_dynamic-update-slice_fusion.12.wa_ref.wd_ref, ...), custom_call_target="tpu_custom_call" | custom-call | flops 10737418240 | bytes 25165824 | tf_op jit(solution)/shard_map/join/pallas_call | solution.py:411
  236.2 11.5 %collective-permute-done.16.other_second = bf16[1024,1024]{1,0:T(8,128)(2,1)} collective-permute-done((bf16[1024,1024]{1,0:T(8,128)(2,1)}, bf16[1024,1024]{1,0:T(8,128)(2,1)}, u32[]{:S(2)}, u32[]{:S(2)}) %collective-permute-start.16) | collective-permute-done | bytes 2097184 | tf_op jit(solution)/shard_map/ppermute | solution.py:638
  247.7 20.1 %part.1 = (bf16[2048,2048]{1,0:T(8,128)(2,1)}, bf16[2048,256]{1,0:T(8,128)(2,1)}, bf16[2048,1024]{1,0:T(8,128)(2,1)}, f32[1,1024]{1,0:T(1,128)}) custom-call(s32[1]{0:T(128)} %bitcast.near_ref, bf16[1024,1024]{1,0:T(8,128)(2,1)} %all-gather.9.cloned.1.call-done.mine_first, bf16[1024,1024]{1,0:T(8,128)(2,1)} %all-gather.11.cloned.1.call-done.mine_second, ...), custom_call_target="tpu_custom_call" | custom-call | flops 10737418240 | bytes 25165824 | tf_op jit(solution)/shard_map/part/pallas_call | solution.py:469
  267.8 24.5 %attend_back.1.tb_ref = bf16[2048,768]{1,0:T(8,128)(2,1)} custom-call(s32[8]{0:T(128)} %and_select_fusion.from_ref, bf16[2048,768]{1,0:T(8,128)(2,1)} %get-tuple-element.84.qkv_ref, bf16[2048,256]{1,0:T(8,128)(2,1)} %get-tuple-element.93.grad_ref, s32[2048,1]{1,0:T(8,128)} %copy.77.begin_ref, f32[2,2048,1]{2,1,0:T(8,128)} %get-tuple-element.94.sum_ref, ...), custom_call_target="tpu_custom_call" | custom-call | flops 10737418240 | bytes 7340032 | tf_op jit(solution)/shard_map/attend_back/pallas_call | solution.py:370
  292.5 4.3 add_convert_fusion.3
  296.8 27.9 %back.1 = (f32[1024,1024]{1,0:T(8,128)}, f32[1024,1024]{1,0:T(8,128)}, bf16[1024,1024]{1,0:T(8,128)(2,1)}, bf16[1024,1024]{1,0:T(8,128)(2,1)}, f32[2048,2]{1,0:T(8,128)}, /*index=5*/f32[4,2048]{1,0:T(4,128)}) custom-call(s32[1]{0:T(128)} %bitcast.near_ref, bf16[2048,768]{1,0:T(8,128)(2,1)} %attend_back.1.tb_ref, ...), custom_call_target="tpu_custom_call" | custom-call | flops 15032385536 | bytes 33554432 | tf_op jit(solution)/shard_map/back/pallas_call | solution.py:565
  324.8 13.2 %fusion.14 = f32[1024,2048]{1,0:T(8,128)S(1)} fusion(bf16[2048,1024]{1,0:T(8,128)(2,1)} %get-tuple-element.86.b_ref, bf16[2048,2048]{1,0:T(8,128)(2,1)} %get-tuple-element.103), kind=kOutput, calls=%fused_computation.87 | convolution fusion | flops 8589934592 | bytes 20971520 | tf_op jit(solution)/shard_map/dot_general | solution.py:35
  340.0 2.4 fusion.13
  342.3 1.5 collective-permute-start.18
  344.6 3.8 add_convert_fusion.2
  350.1 10.6 %collective-permute-start.25 = (bf16[256,512]{1,0:T(8,128)(2,1)S(1)}, bf16[256,512]{1,0:T(8,128)(2,1)S(1)}, u32[]{:S(2)}, u32[]{:S(2)}) collective-permute-start(bf16[256,512]{1,0:T(8,128)(2,1)S(1)} %add_convert_fusion.7), channel_id=1, source_target_pairs={{0,16},{8,24},{16,0},{24,8},{1,17},{9,25},{17,1},{25,9},{2,18},{10... | collective-permute-start | bytes 786440 | tf_op jit(solution)/shard_map/ppermute | solution.py:638
  360.7 2.3 add_convert_fusion.5
  363.3 14.0 %fusion.15 = f32[2048,1024]{1,0:T(8,128)} fusion(bf16[2048,2048]{1,0:T(8,128)(2,1)} %get-tuple-element.108, bf16[2048,1024]{1,0:T(8,128)(2,1)S(1)} %copy-done.35), kind=kOutput, calls=%fused_computation.88 | convolution fusion | flops 8589934592 | bytes 20971520 | tf_op jit(solution)/shard_map/dot_general | solution.py:35
  379.0 10.8 %collective-permute-done.28 = bf16[1024,512]{1,0:T(8,128)(2,1)S(1)} collective-permute-done((bf16[1024,512]{1,0:T(8,128)(2,1)S(1)}, bf16[1024,512]{1,0:T(8,128)(2,1)S(1)}, u32[]{:S(2)}, u32[]{:S(2)}) %collective-permute-start.28) | collective-permute-done | bytes 1048608 | tf_op jit(solution)/shard_map/ppermute | solution.py:638
  389.8 3.5 convert_add_fusion.2.g_ref
  393.3 3.9 add_convert_fusion.1
  397.2 10.9 %fusion.16 = f32[2048,768]{1,0:T(8,128)} fusion(bf16[2048,2048]{1,0:T(8,128)(2,1)} %get-tuple-element.110, bf16[2048,768]{1,0:T(8,128)(2,1)S(1)} %copy-done.10), kind=kOutput, calls=%fused_computation.89 | convolution fusion | flops 6442450944 | bytes 17825792 | tf_op jit(solution)/shard_map/dot_general | solution.py:35
  408.1 3.7 shard_map.571
  411.8 10.8 %shard_map.572 = (f32[1024,512]{1,0:T(8,128)}, f32[8,4,128,128]{3,2,1,0:T(8,128)}, f32[8,4,128,128]{3,2,1,0:T(8,128)}) custom-call(f32[1024,512]{1,0:T(8,128)} %w_ref.5, f32[1024,512]{1,0:T(8,128)} %convert_add_fusion.2.g_ref, f32[8,4,128,128]{3,2,1,0:T(8,128)} %l_ref.5, f32[8,4,128,128]{3,2,1,0:T(8,128)} %r_ref.5, f32[8,4,128,128]{3,2,1,0:T(8,128)} %p_ref.5, ...), custom_call_target="tpu_custom_call" | custom-call | flops 536870912 | bytes 18874368 | tf_op jit(solution)/shard_map/pallas_call | solution.py:621
  422.5 12.5 %collective-permute-done.22 = bf16[1024,1024]{1,0:T(8,128)(2,1)} collective-permute-done((bf16[1024,1024]{1,0:T(8,128)(2,1)}, bf16[1024,1024]{1,0:T(8,128)(2,1)}, u32[]{:S(2)}, u32[]{:S(2)}) %collective-permute-start.22) | collective-permute-done | bytes 2097184 | tf_op jit(solution)/shard_map/ppermute | solution.py:638
  435.1 5.0 add_convert_fusion
  442.2 2.5 convert_reduce_fusion
  446.0 1.5 collective-permute-start.32
  447.6 11.1 %collective-permute-start.41 = (f32[16,128]{1,0:T(8,128)S(1)}, f32[16,128]{1,0:T(8,128)S(1)}, u32[]{:S(2)}, u32[]{:S(2)}) collective-permute-start(f32[16,128]{1,0:T(8,128)S(1)} %fusion.25), channel_id=1, source_target_pairs={{0,16},{8,24},{16,0},{24,8},{1,17},{9,25},{17,1},{25,9},{2,18},{10... | collective-permute-start | bytes 24584 | tf_op jit(solution)/shard_map/ppermute | solution.py:638
  458.7 3.5 dynamic-slice_convert_fusion.1
  463.6 2.7 collective-permute-done.35
  466.9 5.3 collective-permute-done.36
  472.8 3.0 collective-permute-start.34
  475.8 3.3 collective-permute-done.37
  479.1 3.2 dynamic-slice_convert_fusion.5
  483.6 3.0 add_convert_fusion.4
  486.5 2.0 collective-permute-start.31
  488.7 2.7 add_convert_fusion.6
  492.1 20.7 %collective-permute-done.31 = bf16[512,1024]{1,0:T(8,128)(2,1)} collective-permute-done((bf16[512,1024]{1,0:T(8,128)(2,1)}, bf16[512,1024]{1,0:T(8,128)(2,1)}, u32[]{:S(2)}, u32[]{:S(2)}) %collective-permute-start.31) | collective-permute-done | bytes 1048608 | tf_op jit(solution)/shard_map/ppermute | solution.py:638
  512.9 3.9 convert_add_fusion.1.g_ref
  516.7 9.5 %shard_map.574 = (f32[512,1024]{1,0:T(8,128)}, f32[4,8,128,128]{3,2,1,0:T(8,128)}, f32[4,8,128,128]{3,2,1,0:T(8,128)}) custom-call(f32[512,1024]{1,0:T(8,128)} %w_ref.7, f32[512,1024]{1,0:T(8,128)} %convert_add_fusion.1.g_ref, f32[4,8,128,128]{3,2,1,0:T(8,128)} %l_ref.7, f32[4,8,128,128]{3,2,1,0:T(8,128)} %r_ref.7, f32[4,8,128,128]{3,2,1,0:T(8,128)} %p_ref.7, ...), custom_call_target="tpu_custom_call" | custom-call | flops 536870912 | bytes 18874368 | tf_op jit(solution)/shard_map/pallas_call | solution.py:621
  526.2 2.6 collective-permute-done.21
  528.8 3.3 convert_add_fusion.3.g_ref
  532.1 7.8 %shard_map.573 = (f32[512,768]{1,0:T(8,128)}, f32[4,6,128,128]{3,2,1,0:T(8,128)}, f32[4,6,128,128]{3,2,1,0:T(8,128)}) custom-call(f32[512,768]{1,0:T(8,128)} %w_ref.6, f32[512,768]{1,0:T(8,128)} %convert_add_fusion.3.g_ref, f32[4,6,128,128]{3,2,1,0:T(8,128)} %l_ref.6, f32[4,6,128,128]{3,2,1,0:T(8,128)} %r_ref.6, f32[4,6,128,128]{3,2,1,0:T(8,128)} %p_ref.6, ...), custom_call_target="tpu_custom_call" | custom-call | flops 402653184 | bytes 14155776 | tf_op jit(solution)/shard_map/pallas_call | solution.py:621
  540.0 44.5 %reduce-scatter.9.cloned.1.call-done = bf16[1024,256]{1,0:T(8,128)(2,1)} async-done(((bf16[1024,1024]{1,0:T(8,128)(2,1)}), bf16[1024,256]{1,0:T(8,128)(2,1)}) %reduce-scatter.9.cloned.1.call-update) | async-done | bytes 524304 | tf_op jit(solution)/shard_map/reduce_scatter | solution.py:691
  584.5 5.4 fusion.6
  (217 shorter events, 41.3 us)
Async XLA Ops:
  7.2 52.0 %all-gather.5.cloned.1.call-start = ((), (), s32[]{:S(2)}) async-start(), calls=%async_computation.4 | async-start | bytes 2621440 | tf_op jit(solution)/shard_map/all_gather | solution.py:685
  9.6 96.2 %all-gather.7.cloned.1.call-start = ((), (), s32[]{:S(2)}) async-start(), calls=%async_computation.5 | async-start | bytes 2621440 | tf_op jit(solution)/shard_map/all_gather | solution.py:685
  10.4 142.0 %all-gather.9.cloned.1.call-start = ((), (), s32[]{:S(2)}) async-start(), calls=%async_computation.6 | async-start | bytes 2621440 | tf_op jit(solution)/shard_map/all_gather | solution.py:685
  11.5 187.4 %all-gather.11.cloned.1.call-start = ((), (), s32[]{:S(2)}) async-start(), calls=%async_computation.7 | async-start | bytes 2621440 | tf_op jit(solution)/shard_map/all_gather | solution.py:685
  12.4 16.9 %collective-permute-start = (bf16[256,512]{1,0:T(8,128)(2,1)}, bf16[256,512]{1,0:T(8,128)(2,1)S(1)}, u32[]{:S(2)}, u32[]{:S(2)}) collective-permute-start(bf16[256,512]{1,0:T(8,128)(2,1)} %get-tuple-element.157), channel_id=1, source_target_pairs={{0,16},{8,24},{16,0},{24,8},{1,17},{9,25},{17,1},{25,9},{2,18},{10... | collective-permute-start | bytes 786440 | tf_op jit(solution)/shard_map/ppermute | solution.py:638
  15.4 14.0 %collective-permute-start.1 = (bf16[256,512]{1,0:T(8,128)(2,1)}, bf16[256,512]{1,0:T(8,128)(2,1)S(1)}, u32[]{:S(2)}, u32[]{:S(2)}) collective-permute-start(bf16[256,512]{1,0:T(8,128)(2,1)} %get-tuple-element.157), channel_id=1, source_target_pairs={{0,8},{8,0},{16,24},{24,16},{1,9},{9,1},{17,25},{25,17},{2,10},{10... | collective-permute-start | bytes 786440 | tf_op jit(solution)/shard_map/ppermute | solution.py:638
  18.3 20.9 %collective-permute-start.8 = (bf16[512,768]{1,0:T(8,128)(2,1)}, bf16[512,768]{1,0:T(8,128)(2,1)S(1)}, u32[]{:S(2)}, u32[]{:S(2)}) collective-permute-start(bf16[512,768]{1,0:T(8,128)(2,1)} %get-tuple-element.153), channel_id=1, source_target_pairs={{0,16},{8,24},{16,0},{24,8},{1,17},{9,25},{17,1},{25,9},{2,18},{10... | collective-permute-start | bytes 2359304 | tf_op jit(solution)/shard_map/ppermute | solution.py:638
  19.3 24.7 %collective-permute-start.9 = (bf16[512,768]{1,0:T(8,128)(2,1)}, bf16[512,768]{1,0:T(8,128)(2,1)}, u32[]{:S(2)}, u32[]{:S(2)}) collective-permute-start(bf16[512,768]{1,0:T(8,128)(2,1)} %get-tuple-element.153), channel_id=1, source_target_pairs={{0,8},{8,0},{16,24},{24,16},{1,9},{9,1},{17,25},{25,17},{2,10},{10... | collective-permute-start | bytes 2359304 | tf_op jit(solution)/shard_map/ppermute | solution.py:638
  23.6 38.1 %collective-permute-start.3 = (bf16[1024,512]{1,0:T(8,128)(2,1)}, bf16[1024,512]{1,0:T(8,128)(2,1)}, u32[]{:S(2)}, u32[]{:S(2)}) collective-permute-start(bf16[1024,512]{1,0:T(8,128)(2,1)} %get-tuple-element.155), channel_id=1, source_target_pairs={{0,16},{8,24},{16,0},{24,8},{1,17},{9,25},{17,1},{25,9},{2,18},{10... | collective-permute-start | bytes 3145736 | tf_op jit(solution)/shard_map/ppermute | solution.py:638
  24.7 515.2 %reduce-scatter.7.cloned.1.call-start = ((), (), s32[]{:S(2)}) async-start(), calls=%async_computation.9 | async-start | bytes 2621440 | tf_op jit(solution)/shard_map/reduce_scatter | solution.py:691
  29.3 1.6 collective-permute-start.2
  29.5 9.8 %copy-start.18 = (bf16[256,512]{1,0:T(8,128)(2,1)}, bf16[256,512]{1,0:T(8,128)(2,1)S(1)}, u32[]{:S(2)}) copy-start(bf16[256,512]{1,0:T(8,128)(2,1)S(1)} %collective-permute-done.1) | copy-start | bytes 786436
  29.5 83.4 %collective-permute-start.4 = (bf16[1024,512]{1,0:T(8,128)(2,1)}, bf16[1024,512]{1,0:T(8,128)(2,1)}, u32[]{:S(2)}, u32[]{:S(2)}) collective-permute-start(bf16[1024,512]{1,0:T(8,128)(2,1)} %get-tuple-element.155), channel_id=1, source_target_pairs={{0,8},{8,0},{16,24},{24,16},{1,9},{9,1},{17,25},{25,17},{2,10},{10... | collective-permute-start | bytes 3145736 | tf_op jit(solution)/shard_map/ppermute | solution.py:638
  30.9 83.6 %collective-permute-start.11 = (bf16[512,1024]{1,0:T(8,128)(2,1)}, bf16[512,1024]{1,0:T(8,128)(2,1)}, u32[]{:S(2)}, u32[]{:S(2)}) collective-permute-start(bf16[512,1024]{1,0:T(8,128)(2,1)} %get-tuple-element.151), channel_id=1, source_target_pairs={{0,16},{8,24},{16,0},{24,8},{1,17},{9,25},{17,1},{25,9},{2,18},{10... | collective-permute-start | bytes 3145736 | tf_op jit(solution)/shard_map/ppermute | solution.py:638
  40.1 74.9 %collective-permute-start.12 = (bf16[512,1024]{1,0:T(8,128)(2,1)}, bf16[512,1024]{1,0:T(8,128)(2,1)}, u32[]{:S(2)}, u32[]{:S(2)}) collective-permute-start(bf16[512,1024]{1,0:T(8,128)(2,1)} %get-tuple-element.151), channel_id=1, source_target_pairs={{0,8},{8,0},{16,24},{24,16},{1,9},{9,1},{17,25},{25,17},{2,10},{10... | collective-permute-start | bytes 3145736 | tf_op jit(solution)/shard_map/ppermute | solution.py:638
  59.2 94.7 %collective-permute-start.6 = (bf16[1024,1024]{1,0:T(8,128)(2,1)}, bf16[1024,1024]{1,0:T(8,128)(2,1)}, u32[]{:S(2)}, u32[]{:S(2)}) collective-permute-start(bf16[1024,1024]{1,0:T(8,128)(2,1)} %all-gather.5.cloned.1.call-done.mine_first), channel_id=1, source_target_pairs={{0,1},{1,0},{2,3},{3,2},{4,5},{5,4},{6,7},{7,6},{8,9},{9,8},{10,11... | collective-permute-start | bytes 6291464 | tf_op jit(solution)/shard_map/ppermute | solution.py:638
  105.8 48.1 %collective-permute-start.7 = (bf16[1024,1024]{1,0:T(8,128)(2,1)}, bf16[1024,1024]{1,0:T(8,128)(2,1)}, u32[]{:S(2)}, u32[]{:S(2)}) collective-permute-start(bf16[1024,1024]{1,0:T(8,128)(2,1)} %all-gather.7.cloned.1.call-done.mine_second), channel_id=1, source_target_pairs={{0,1},{1,0},{2,3},{3,2},{4,5},{5,4},{6,7},{7,6},{8,9},{9,8},{10,11... | collective-permute-start | bytes 6291464 | tf_op jit(solution)/shard_map/ppermute | solution.py:638
  112.8 15.5 %collective-permute-start.5 = (bf16[1024,512]{1,0:T(8,128)(2,1)}, bf16[1024,512]{1,0:T(8,128)(2,1)S(1)}, u32[]{:S(2)}, u32[]{:S(2)}) collective-permute-start(bf16[1024,512]{1,0:T(8,128)(2,1)} %collective-permute-done.3), channel_id=1, source_target_pairs={{0,8},{8,0},{16,24},{24,16},{1,9},{9,1},{17,25},{25,17},{2,10},{10... | collective-permute-start | bytes 3145736 | tf_op jit(solution)/shard_map/ppermute | solution.py:638
  114.5 12.9 %collective-permute-start.10 = (bf16[512,768]{1,0:T(8,128)(2,1)}, bf16[512,768]{1,0:T(8,128)(2,1)S(1)}, u32[]{:S(2)}, u32[]{:S(2)}) collective-permute-start(bf16[512,768]{1,0:T(8,128)(2,1)} %copy-done.16), channel_id=1, source_target_pairs={{0,8},{8,0},{16,24},{24,16},{1,9},{9,1},{17,25},{25,17},{2,10},{10... | collective-permute-start | bytes 2359304 | tf_op jit(solution)/shard_map/ppermute | solution.py:638
  115.0 14.4 %collective-permute-start.13 = (bf16[512,1024]{1,0:T(8,128)(2,1)}, bf16[512,1024]{1,0:T(8,128)(2,1)S(1)}, u32[]{:S(2)}, u32[]{:S(2)}) collective-permute-start(bf16[512,1024]{1,0:T(8,128)(2,1)} %collective-permute-done.11), channel_id=1, source_target_pairs={{0,8},{8,0},{16,24},{24,16},{1,9},{9,1},{17,25},{25,17},{2,10},{10... | collective-permute-start | bytes 3145736 | tf_op jit(solution)/shard_map/ppermute | solution.py:638
  152.4 83.8 %collective-permute-start.15 = (bf16[1024,1024]{1,0:T(8,128)(2,1)}, bf16[1024,1024]{1,0:T(8,128)(2,1)}, u32[]{:S(2)}, u32[]{:S(2)}) collective-permute-start(bf16[1024,1024]{1,0:T(8,128)(2,1)} %all-gather.9.cloned.1.call-done.mine_first), channel_id=1, source_target_pairs={{0,1},{1,0},{2,3},{3,2},{4,5},{5,4},{6,7},{7,6},{8,9},{9,8},{10,11... | collective-permute-start | bytes 6291464 | tf_op jit(solution)/shard_map/ppermute | solution.py:638
  198.9 48.8 %collective-permute-start.16 = (bf16[1024,1024]{1,0:T(8,128)(2,1)}, bf16[1024,1024]{1,0:T(8,128)(2,1)}, u32[]{:S(2)}, u32[]{:S(2)}) collective-permute-start(bf16[1024,1024]{1,0:T(8,128)(2,1)} %all-gather.11.cloned.1.call-done.mine_second), channel_id=1, source_target_pairs={{0,1},{1,0},{2,3},{3,2},{4,5},{5,4},{6,7},{7,6},{8,9},{9,8},{10,11... | collective-permute-start | bytes 6291464 | tf_op jit(solution)/shard_map/ppermute | solution.py:638
  234.2 58.3 %collective-permute-start.14 = (bf16[1024,1024]{1,0:T(8,128)(2,1)}, bf16[1024,1024]{1,0:T(8,128)(2,1)S(1)}, u32[]{:S(2)}, u32[]{:S(2)}) collective-permute-start(bf16[1024,1024]{1,0:T(8,128)(2,1)} %get-tuple-element.88), channel_id=1, source_target_pairs={{0,1},{1,0},{2,3},{3,2},{4,5},{5,4},{6,7},{7,6},{8,9},{9,8},{10,11... | collective-permute-start | bytes 6291464 | tf_op jit(solution)/shard_map/ppermute | solution.py:638
  234.8 109.0 %collective-permute-start.17 = (bf16[1024,1024]{1,0:T(8,128)(2,1)}, bf16[1024,1024]{1,0:T(8,128)(2,1)}, u32[]{:S(2)}, u32[]{:S(2)}) collective-permute-start(bf16[1024,1024]{1,0:T(8,128)(2,1)} %get-tuple-element.97), channel_id=1, source_target_pairs={{0,1},{1,0},{2,3},{3,2},{4,5},{5,4},{6,7},{7,6},{8,9},{9,8},{10,11... | collective-permute-start | bytes 6291464 | tf_op jit(solution)/shard_map/ppermute | solution.py:638
  324.8 14.5 %slice-start = ((s8[8388608]{0:T(1024)(128)(4,1)}), s8[4194304]{0:T(1024)(128)(4,1)S(1)}, s32[]{:S(2)}) async-start(s8[8388608]{0:T(1024)(128)(4,1)} %bitcast.42), calls=%async_computation.12 | async-start | bytes 8388608
  324.8 14.5 %slice-start.1 = ((s8[8388608]{0:T(1024)(128)(4,1)}), s8[4194304]{0:T(1024)(128)(4,1)S(1)}, s32[]{:S(2)}) async-start(s8[8388608]{0:T(1024)(128)(4,1)} %bitcast.42), calls=%async_computation.13 | async-start | bytes 8388608
  339.3 21.4 %collective-permute-start.27 = (bf16[1024,512]{1,0:T(8,128)(2,1)}, bf16[1024,512]{1,0:T(8,128)(2,1)}, u32[]{:S(2)}, u32[]{:S(2)}) collective-permute-start(bf16[1024,512]{1,0:T(8,128)(2,1)} %get-tuple-element.161), channel_id=1, source_target_pairs={{0,8},{8,0},{16,24},{24,16},{1,9},{9,1},{17,25},{25,17},{2,10},{10... | collective-permute-start | bytes 3145736 | tf_op jit(solution)/shard_map/ppermute | solution.py:638
  342.3 50.9 %collective-permute-start.18 = (bf16[1024,1024]{1,0:T(8,128)(2,1)}, bf16[1024,1024]{1,0:T(8,128)(2,1)}, u32[]{:S(2)}, u32[]{:S(2)}) collective-permute-start(bf16[1024,1024]{1,0:T(8,128)(2,1)} %get-tuple-element.102), channel_id=1, source_target_pairs={{0,1},{1,0},{2,3},{3,2},{4,5},{5,4},{6,7},{7,6},{8,9},{9,8},{10,11... | collective-permute-start | bytes 6291464 | tf_op jit(solution)/shard_map/ppermute | solution.py:638
  344.6 4.5 collective-permute-start.24
  348.4 191.5 %reduce-scatter.11.cloned.1.call-start = ((), (), s32[]{:S(2)}) async-start(), calls=%async_computation.11 | async-start | bytes 2621440 | tf_op jit(solution)/shard_map/reduce_scatter | solution.py:691
  348.4 30.6 %collective-permute-start.26 = (bf16[1024,512]{1,0:T(8,128)(2,1)S(1)}, bf16[1024,512]{1,0:T(8,128)(2,1)S(1)}, u32[]{:S(2)}, u32[]{:S(2)}) collective-permute-start(bf16[1024,512]{1,0:T(8,128)(2,1)S(1)} %get-tuple-element.160), channel_id=1, source_target_pairs={{0,8},{8,0},{16,24},{24,16},{1,9},{9,1},{17,25},{25,17},{2,10},{10... | collective-permute-start | bytes 3145736 | tf_op jit(solution)/shard_map/ppermute | solution.py:638
  349.0 28.3 %collective-permute-start.23 = (bf16[256,512]{1,0:T(8,128)(2,1)S(1)}, bf16[256,512]{1,0:T(8,128)(2,1)S(1)}, u32[]{:S(2)}, u32[]{:S(2)}) collective-permute-start(bf16[256,512]{1,0:T(8,128)(2,1)S(1)} %get-tuple-element.164), channel_id=1, source_target_pairs={{0,8},{8,0},{16,24},{24,16},{1,9},{9,1},{17,25},{25,17},{2,10},{10... | collective-permute-start | bytes 786440 | tf_op jit(solution)/shard_map/ppermute | solution.py:638
  350.1 13.2 %copy-start.35 = (bf16[2048,1024]{1,0:T(8,128)(2,1)S(1)}, bf16[2048,1024]{1,0:T(8,128)(2,1)}, u32[]{:S(2)}) copy-start(bf16[2048,1024]{1,0:T(8,128)(2,1)} %get-tuple-element.100.hb_ref) | copy-start | bytes 12582916
  350.1 28.0 %collective-permute-start.25 = (bf16[256,512]{1,0:T(8,128)(2,1)S(1)}, bf16[256,512]{1,0:T(8,128)(2,1)S(1)}, u32[]{:S(2)}, u32[]{:S(2)}) collective-permute-start(bf16[256,512]{1,0:T(8,128)(2,1)S(1)} %add_convert_fusion.7), channel_id=1, source_target_pairs={{0,16},{8,24},{16,0},{24,8},{1,17},{9,25},{17,1},{25,9},{2,18},{10... | collective-permute-start | bytes 786440 | tf_op jit(solution)/shard_map/ppermute | solution.py:638
  363.1 26.7 %collective-permute-start.28 = (bf16[1024,512]{1,0:T(8,128)(2,1)S(1)}, bf16[1024,512]{1,0:T(8,128)(2,1)S(1)}, u32[]{:S(2)}, u32[]{:S(2)}) collective-permute-start(bf16[1024,512]{1,0:T(8,128)(2,1)S(1)} %add_convert_fusion.5), channel_id=1, source_target_pairs={{0,16},{8,24},{16,0},{24,8},{1,17},{9,25},{17,1},{25,9},{2,18},{10... | collective-permute-start | bytes 3145736 | tf_op jit(solution)/shard_map/ppermute | solution.py:638
  377.3 57.7 %collective-permute-start.22 = (bf16[1024,1024]{1,0:T(8,128)(2,1)}, bf16[1024,1024]{1,0:T(8,128)(2,1)}, u32[]{:S(2)}, u32[]{:S(2)}) collective-permute-start(bf16[1024,1024]{1,0:T(8,128)(2,1)} %get-tuple-element.112), channel_id=1, source_target_pairs={{0,1},{1,0},{2,3},{3,2},{4,5},{5,4},{6,7},{7,6},{8,9},{9,8},{10,11... | collective-permute-start | bytes 6291464 | tf_op jit(solution)/shard_map/ppermute | solution.py:638
  379.0 14.3 %copy-start.7 = (f32[1024,1024]{1,0:T(8,128)S(1)}, f32[1024,1024]{1,0:T(8,128)}, u32[]{:S(2)}) copy-start(f32[1024,1024]{1,0:T(8,128)} %get-tuple-element.106) | copy-start | bytes 12582916
  440.1 99.9 %reduce-scatter.5.cloned.1.call-start = ((), (), s32[]{:S(2)}) async-start(), calls=%async_computation.8 | async-start | bytes 2621440 | tf_op jit(solution)/shard_map/reduce_scatter | solution.py:691
  440.8 143.6 %reduce-scatter.9.cloned.1.call-start = ((), (), s32[]{:S(2)}) async-start(), calls=%async_computation.10 | async-start | bytes 2621440 | tf_op jit(solution)/shard_map/reduce_scatter | solution.py:691
  444.7 2.9 collective-permute-start.40
  446.0 17.4 %collective-permute-start.32 = (f32[32,128]{1,0:T(8,128)S(1)}, f32[32,128]{1,0:T(8,128)S(1)}, u32[]{:S(2)}, u32[]{:S(2)}) collective-permute-start(f32[32,128]{1,0:T(8,128)S(1)} %reshape.162), channel_id=1, source_target_pairs={{0,1},{1,0},{2,3},{3,2},{4,5},{5,4},{6,7},{7,6},{8,9},{9,8},{10,11... | collective-permute-start | bytes 49160 | tf_op jit(solution)/shard_map/ppermute | solution.py:638
  447.5 14.7 %copy-start.21 = (f32[4,2048]{1,0:T(4,128)S(1)}, f32[4,2048]{1,0:T(4,128)}, u32[]{:S(2)}) copy-start(f32[4,2048]{1,0:T(4,128)} %get-tuple-element.133) | copy-start | bytes 98308
  447.5 18.7 %copy-start.27 = (f32[1024]{0:T(1024)S(1)}, f32[1024]{0:T(1024)}, u32[]{:S(2)}) copy-start(f32[1024]{0:T(1024)} %param.47) | copy-start | bytes 12292
  447.6 18.7 %copy-start.28 = (f32[1024]{0:T(1024)S(1)}, f32[1024]{0:T(1024)}, u32[]{:S(2)}) copy-start(f32[1024]{0:T(1024)} %param.54) | copy-start | bytes 12292
  447.6 18.7 %copy-start.29 = (f32[1024]{0:T(1024)S(1)}, f32[1024]{0:T(1024)}, u32[]{:S(2)}) copy-start(f32[1024]{0:T(1024)} %param.55) | copy-start | bytes 12292
  447.6 24.6 %copy-start.30 = (f32[768]{0:T(1024)S(1)}, f32[768]{0:T(1024)}, u32[]{:S(2)}) copy-start(f32[768]{0:T(1024)} %param.50) | copy-start | bytes 9220
  447.6 24.6 %copy-start.31 = (f32[768]{0:T(1024)S(1)}, f32[768]{0:T(1024)}, u32[]{:S(2)}) copy-start(f32[768]{0:T(1024)} %param.51) | copy-start | bytes 9220
  447.6 15.9 %collective-permute-start.41 = (f32[16,128]{1,0:T(8,128)S(1)}, f32[16,128]{1,0:T(8,128)S(1)}, u32[]{:S(2)}, u32[]{:S(2)}) collective-permute-start(f32[16,128]{1,0:T(8,128)S(1)} %fusion.25), channel_id=1, source_target_pairs={{0,16},{8,24},{16,0},{24,8},{1,17},{9,25},{17,1},{25,9},{2,18},{10... | collective-permute-start | bytes 24584 | tf_op jit(solution)/shard_map/ppermute | solution.py:638
  462.2 20.6 %copy-start.32 = (f32[2,256]{1,0:T(2,128)S(1)}, f32[2,256]{1,0:T(2,128)}, u32[]{:S(2)}) copy-start(f32[2,256]{1,0:T(2,128)} %param.52) | copy-start | bytes 6148
  462.2 20.6 %copy-start.33 = (f32[2,256]{1,0:T(2,128)S(1)}, f32[2,256]{1,0:T(2,128)}, u32[]{:S(2)}) copy-start(f32[2,256]{1,0:T(2,128)} %param.53) | copy-start | bytes 6148
  462.3 4.0 collective-permute-start.35
  462.9 20.6 %collective-permute-start.30 = (bf16[512,1024]{1,0:T(8,128)(2,1)}, bf16[512,1024]{1,0:T(8,128)(2,1)S(1)}, u32[]{:S(2)}, u32[]{:S(2)}) collective-permute-start(bf16[512,1024]{1,0:T(8,128)(2,1)} %get-tuple-element.159), channel_id=1, source_target_pairs={{0,8},{8,0},{16,24},{24,16},{1,9},{9,1},{17,25},{25,17},{2,10},{10... | collective-permute-start | bytes 3145736 | tf_op jit(solution)/shard_map/ppermute | solution.py:638
  462.9 29.2 %collective-permute-start.29 = (bf16[512,1024]{1,0:T(8,128)(2,1)S(1)}, bf16[512,1024]{1,0:T(8,128)(2,1)S(1)}, u32[]{:S(2)}, u32[]{:S(2)}) collective-permute-start(bf16[512,1024]{1,0:T(8,128)(2,1)S(1)} %get-tuple-element.158), channel_id=1, source_target_pairs={{0,8},{8,0},{16,24},{24,16},{1,9},{9,1},{17,25},{25,17},{2,10},{10... | collective-permute-start | bytes 3145736 | tf_op jit(solution)/shard_map/ppermute | solution.py:638
  463.5 9.4 %collective-permute-start.33 = (f32[32,128]{1,0:T(8,128)S(1)}, f32[32,128]{1,0:T(8,128)S(1)}, u32[]{:S(2)}, u32[]{:S(2)}) collective-permute-start(f32[32,128]{1,0:T(8,128)S(1)} %add.228), channel_id=1, source_target_pairs={{0,2},{2,0},{4,6},{6,4},{1,3},{3,1},{5,7},{7,5},{8,10},{10,8},{12,... | collective-permute-start | bytes 49160 | tf_op jit(solution)/shard_map/ppermute | solution.py:638
  466.2 5.9 collective-permute-start.36
  472.2 6.9 %collective-permute-start.37 = (f32[64,128]{1,0:T(8,128)S(1)}, f32[64,128]{1,0:T(8,128)S(1)}, u32[]{:S(2)}, u32[]{:S(2)}) collective-permute-start(f32[64,128]{1,0:T(8,128)S(1)} %add.233), channel_id=1, source_target_pairs={{0,4},{2,6},{4,0},{6,2},{1,5},{3,7},{5,1},{7,3},{8,12},{10,14},{12... | collective-permute-start | bytes 98312 | tf_op jit(solution)/shard_map/ppermute | solution.py:638
  472.8 10.6 %collective-permute-start.34 = (f32[32,128]{1,0:T(8,128)S(1)}, f32[32,128]{1,0:T(8,128)S(1)}, u32[]{:S(2)}, u32[]{:S(2)}) collective-permute-start(f32[32,128]{1,0:T(8,128)S(1)} %add.229), channel_id=1, source_target_pairs={{0,4},{2,6},{4,0},{6,2},{1,5},{3,7},{5,1},{7,3},{8,12},{10,14},{12... | collective-permute-start | bytes 49160 | tf_op jit(solution)/shard_map/ppermute | solution.py:638
  479.1 4.3 collective-permute-start.38
  482.4 6.3 %collective-permute-start.20 = (bf16[512,768]{1,0:T(8,128)(2,1)}, bf16[512,768]{1,0:T(8,128)(2,1)}, u32[]{:S(2)}, u32[]{:S(2)}) collective-permute-start(bf16[512,768]{1,0:T(8,128)(2,1)} %get-tuple-element.163), channel_id=1, source_target_pairs={{0,8},{8,0},{16,24},{24,16},{1,9},{9,1},{17,25},{25,17},{2,10},{10... | collective-permute-start | bytes 2359304 | tf_op jit(solution)/shard_map/ppermute | solution.py:638
  483.5 5.1 collective-permute-start.39
  486.5 26.3 %collective-permute-start.31 = (bf16[512,1024]{1,0:T(8,128)(2,1)}, bf16[512,1024]{1,0:T(8,128)(2,1)}, u32[]{:S(2)}, u32[]{:S(2)}) collective-permute-start(bf16[512,1024]{1,0:T(8,128)(2,1)} %add_convert_fusion.4), channel_id=1, source_target_pairs={{0,16},{8,24},{16,0},{24,8},{1,17},{9,25},{17,1},{25,9},{2,18},{10... | collective-permute-start | bytes 3145736 | tf_op jit(solution)/shard_map/ppermute | solution.py:638
  488.6 37.6 %collective-permute-start.19 = (bf16[512,768]{1,0:T(8,128)(2,1)}, bf16[512,768]{1,0:T(8,128)(2,1)}, u32[]{:S(2)}, u32[]{:S(2)}) collective-permute-start(bf16[512,768]{1,0:T(8,128)(2,1)} %get-tuple-element.162), channel_id=1, source_target_pairs={{0,8},{8,0},{16,24},{24,16},{1,9},{9,1},{17,25},{25,17},{2,10},{10... | collective-permute-start | bytes 2359304 | tf_op jit(solution)/shard_map/ppermute | solution.py:638
  491.4 37.4 %collective-permute-start.21 = (bf16[512,768]{1,0:T(8,128)(2,1)}, bf16[512,768]{1,0:T(8,128)(2,1)}, u32[]{:S(2)}, u32[]{:S(2)}) collective-permute-start(bf16[512,768]{1,0:T(8,128)(2,1)} %add_convert_fusion.6), channel_id=1, source_target_pairs={{0,16},{8,24},{16,0},{24,8},{1,17},{9,25},{17,1},{25,9},{2,18},{10... | collective-permute-start | bytes 2359304 | tf_op jit(solution)/shard_map/ppermute | solution.py:638
  532.1 52.4 %copy-start.6 = (bf16[2048,256]{1,0:T(8,128)(2,1)S(1)}, bf16[2048,256]{1,0:T(8,128)(2,1)}, u32[]{:S(2)}) copy-start(bf16[2048,256]{1,0:T(8,128)(2,1)} %param.36) | copy-start | bytes 3145732
  (24 other events, 82.2 us)
Sparse Core Ops, SparseCore 0:
  10.2 48.9 all-gather.4
  61.3 44.4 all-gather.6
  107.9 44.4 all-gather.8
  154.4 44.4 all-gather.10
  348.5 50.0 reduce-scatter.6
  440.2 53.3 reduce-scatter.10
  495.9 42.8 reduce-scatter.4
  541.6 42.7 reduce-scatter.8
